TPU v7x, 32 devices: a whole 2x2x4 slice. The times are simulated.
32 devices in a mesh: lat: 4 (over y, x), lon: 8 (over z, core).
Axes of the slice: x: 2, y: 2, z: 4, core: 2. Of those that a mesh axis runs over, the one named last changes fastest.
Arguments:
- pressure: float32 [4, 30, 5120], P('lat', None, 'lon'), may hold values from -6 to 6
- velocity: float32 [4, 30, 7680], P('lat', None, 'lon'), may hold values from -6 to 6
- edge_cells: int32 [4, 2, 7680], P('lat', None, 'lon'), may hold values from 0 to 1663
- cell_edges: int32 [4, 3, 5120], P('lat', None, 'lon'), may hold values from 0 to 1983
- send_cells: int32 [4, 8, 1024], P('lat', None, 'lon'), may hold values from 0 to 639
- send_edges: int32 [4, 8, 1024], P('lat', None, 'lon'), may hold values from 0 to 959
- inv_dual: float32 [4, 7680], P('lat', 'lon'), may hold values from 0.5 to 2
- edge_weight: float32 [4, 3, 5120], P('lat', None, 'lon'), may hold values from -3 to 3
- sound_speed: float32 [4, 5120], P('lat', 'lon'), may hold values from 0.1 to 0.6
- coupling: float32 [4, 30, 5120], P('lat', None, 'lon'), may hold values from 0.1 to 2
Outputs:
- pressure_out: float32 [4, 30, 5120], P('lat', None, 'lon')
- velocity_out: float32 [4, 30, 7680], P('lat', None, 'lon')
Inputs may be any that keep to these rules, and one draw needn't show every extreme that they name: `edge_cells`: positions below 640 are own cells; position 640 + r * 128 + j is slot j of the halo piece from the neighbour at offset number r. `cell_edges`: positions below 960 are own edges; position 960 + r * 128 + j is slot j of the edge halo piece from the neighbour at offset number r. `send_cells`: indices of own cells. `send_edges`: indices of own edges.
All inputs are finite; a program needn't handle non-finite values.
Results may differ from a plain program's by a relative error of at most 0.0001.
Values sent between devices are 32-bit elements; how exact they have to be, the bound alone decides.
A program may use at most 64 MiB of HBM per device.

v0:
```python
import jax
import jax.numpy as jnp
from jax import lax
from jax.sharding import PartitionSpec as P

NSUB = 3


DIRECTIONS = ((-1, -1), (-1, 0), (-1, 1), (0, -1), (0, 1), (1, -1), (1, 0), (1, 1))
step_scale = 0.5


def from_behind(block, axis, distance):
    devices = range(lax.axis_size(axis))
    route = [((i - distance) % len(devices), i) for i in devices]
    return lax.ppermute(block, axis, route)


def passed_along(value, axis, steps):
    count = lax.axis_size(axis)
    first, last = (max(0, -steps), min(count, count - steps))
    return lax.ppermute(value, axis, [(source, source + steps) for source in range(first, last)])


def position(offset):
    return DIRECTIONS.index(offset)


def edge_update(normal, extended, edge_cells, inv_dual):
    gradient = (
        jnp.take(extended, edge_cells[1], axis=1) - jnp.take(extended, edge_cells[0], axis=1)
    ) * inv_dual[None, :]
    return normal - step_scale * gradient


def column_solve(right_side, coupling):
    levels = right_side.shape[0]
    ratios = []
    scaled = []
    for level_index in range(levels):
        if level_index < levels - 1:
            upper_term = -coupling[level_index]
        else:
            upper_term = 0.0 * coupling[0]
        if level_index == 0:
            divisor = 1.0 + coupling[0]
            current = right_side[0] / divisor
        else:
            lower_term = -coupling[level_index - 1]
            diagonal = 1.0 + coupling[level_index - 1] + coupling[level_index]
            divisor = diagonal - lower_term * ratios[-1]
            current = (right_side[level_index] - lower_term * scaled[-1]) / divisor
        ratios.append(upper_term / divisor)
        scaled.append(current)
    result = [scaled[-1]]
    for level_index in range(levels - 2, -1, -1):
        result.insert(0, scaled[level_index] - ratios[level_index] * result[0])
    return jnp.stack(result)


def cell_update(values, edges_ext, cell_edges, edge_weight, sound_speed, coupling):
    divergence = jnp.take(edges_ext, cell_edges[0], axis=1) * edge_weight[0][None, :]
    divergence = divergence + jnp.take(edges_ext, cell_edges[1], axis=1) * edge_weight[1][None, :]
    divergence = divergence + jnp.take(edges_ext, cell_edges[2], axis=1) * edge_weight[2][None, :]
    right_side = values - sound_speed[None, :] * divergence
    return column_solve(right_side, coupling)


def extend(source, send_list):
    buffers = [jnp.take(source, send_list[member], axis=1) for member in range(8)]
    received = {}
    passing = {}
    for lon_step in (1, -1):
        bundle = jnp.stack([buffers[position((lat_step, lon_step))] for lat_step in (-1, 0, 1)])
        arrived = from_behind(bundle, "lon", lon_step)
        received[0, -lon_step] = arrived[1]
        passing[-1, lon_step] = arrived[0]
        passing[1, lon_step] = arrived[2]
    for lat_step in (1, -1):
        bundle = jnp.stack(
            [passing[lat_step, -1], buffers[position((lat_step, 0))], passing[lat_step, 1]]
        )
        arrived = passed_along(bundle, "lat", lat_step)
        for member, lon_step in enumerate((-1, 0, 1)):
            received[-lat_step, -lon_step] = arrived[member]
    return jnp.concatenate([source] + [received[offset] for offset in DIRECTIONS], axis=1)


def on_device(
    pressure,
    velocity,
    edge_cells,
    cell_edges,
    send_cells,
    send_edges,
    inv_dual,
    edge_weight,
    sound_speed,
    coupling,
):
    values = pressure[0]
    normal = velocity[0]
    for substep in range(NSUB):
        extended = extend(values, send_cells[0])
        normal = edge_update(normal, extended, edge_cells[0], inv_dual[0])
        edges_ext = extend(normal, send_edges[0])
        values = cell_update(
            values, edges_ext, cell_edges[0], edge_weight[0], sound_speed[0], coupling[0]
        )
    return (values[None], normal[None])


def solution(mesh):
    return jax.shard_map(
        on_device,
        mesh=mesh,
        in_specs=(
            P("lat", None, "lon"),
            P("lat", None, "lon"),
            P("lat", None, "lon"),
            P("lat", None, "lon"),
            P("lat", None, "lon"),
            P("lat", None, "lon"),
            P("lat", "lon"),
            P("lat", None, "lon"),
            P("lat", "lon"),
            P("lat", None, "lon"),
        ),
        out_specs=(P("lat", None, "lon"), P("lat", None, "lon")),
        check_vma=False,
    )
```

profile of v0, /device:TPU:0, one launch (start us, length us, event | category | flops | bytes accessed | tf_op | source)
XLA Modules:
  0.0 204.7 jit_solution(5628865552744668317)
XLA Ops:
  0.6 1.1 copy.961
  7.0 4.1 %collective-permute-start = (f32[3,30,128]{2,1,0:T(8,128)S(1)}, f32[3,30,128]{2,1,0:T(8,128)S(1)}, u32[]{:S(2)}, u32[]{:S(2)}) collective-permute-start(f32[3,30,128]{2,1,0:T(8,128)S(1)} %pad_maximum_fusion.12), channel_id=1, source_target_pairs={{1,0},{2,1},{3,2},{4,3},{5,4},{6,5},{7,6},{0,7},{9,8},{10,9},{11,1... | collective-permute-start | bytes 138248 | tf_op jit(solution)/shard_map/ppermute | solution.py:16
  18.2 3.9 %collective-permute-start.2 = (f32[3,30,128]{2,1,0:T(8,128)S(1)}, f32[3,30,128]{2,1,0:T(8,128)S(1)}, u32[]{:S(2)}, u32[]{:S(2)}) collective-permute-start(f32[3,30,128]{2,1,0:T(8,128)S(1)} %pad_maximum_fusion.14), channel_id=1, source_target_pairs={{0,8},{8,16},{16,24},{1,9},{9,17},{17,25},{2,10},{10,18},{18,26},{... | collective-permute-start | bytes 138248 | tf_op jit(solution)/shard_map/ppermute | solution.py:22
  22.1 1.3 collective-permute-start.3
  23.8 4.2 %collective-permute-done.3 = f32[3,30,128]{2,1,0:T(8,128)S(1)} collective-permute-done((f32[3,30,128]{2,1,0:T(8,128)S(1)}, f32[3,30,128]{2,1,0:T(8,128)S(1)}, u32[]{:S(2)}, u32[]{:S(2)}) %collective-permute-start.3) | collective-permute-done | bytes 46112 | tf_op jit(solution)/shard_map/ppermute | solution.py:22
  28.4 2.9 %gather_fusion.9 = f32[960,30]{1,0:T(8,128)S(1)} fusion(f32[30,1664]{0,1:T(8,128)S(1)} %copy.911, s32[1024]{0:T(1024)S(1)} %pad_clamp_fusion.11), kind=kCustom, calls=%fused_computation.27.clone | custom fusion | bytes 234240 | tf_op jit(solution)/shard_map/jit(_take)/gather | solution.py:31
  31.3 2.9 %gather_fusion.8 = f32[960,30]{1,0:T(8,128)S(1)} fusion(f32[30,1664]{0,1:T(8,128)S(1)} %copy.911, s32[1024]{0:T(1024)S(1)} %pad_clamp_fusion.12), kind=kCustom, calls=%fused_computation.1.clone | custom fusion | bytes 234240 | tf_op jit(solution)/shard_map/jit(_take)/gather | solution.py:31
  40.4 3.6 %collective-permute-start.4 = (f32[3,30,128]{1,2,0:T(8,128)S(1)}, f32[3,30,128]{1,2,0:T(8,128)S(1)}, u32[]{:S(2)}, u32[]{:S(2)}) collective-permute-start(f32[3,30,128]{1,2,0:T(8,128)S(1)} %pad_maximum_fusion), channel_id=1, source_target_pairs={{1,0},{2,1},{3,2},{4,3},{5,4},{6,5},{7,6},{0,7},{9,8},{10,9},{11,1... | collective-permute-start | bytes 138248 | tf_op jit(solution)/shard_map/ppermute | solution.py:16
  44.8 2.3 %collective-permute-done.4 = f32[3,30,128]{1,2,0:T(8,128)S(1)} collective-permute-done((f32[3,30,128]{1,2,0:T(8,128)S(1)}, f32[3,30,128]{1,2,0:T(8,128)S(1)}, u32[]{:S(2)}, u32[]{:S(2)}) %collective-permute-start.4) | collective-permute-done | bytes 46112 | tf_op jit(solution)/shard_map/ppermute | solution.py:16
  47.2 4.3 %collective-permute-start.6 = (f32[3,30,128]{1,2,0:T(8,128)S(1)}, f32[3,30,128]{1,2,0:T(8,128)S(1)}, u32[]{:S(2)}, u32[]{:S(2)}) collective-permute-start(f32[3,30,128]{1,2,0:T(8,128)S(1)} %pad_maximum_fusion.2), channel_id=1, source_target_pairs={{0,8},{8,16},{16,24},{1,9},{9,17},{17,25},{2,10},{10,18},{18,26},{... | collective-permute-start | bytes 138248 | tf_op jit(solution)/shard_map/ppermute | solution.py:22
  51.5 1.3 collective-permute-start.7
  52.8 2.1 %collective-permute-done.6 = f32[3,30,128]{1,2,0:T(8,128)S(1)} collective-permute-done((f32[3,30,128]{1,2,0:T(8,128)S(1)}, f32[3,30,128]{1,2,0:T(8,128)S(1)}, u32[]{:S(2)}, u32[]{:S(2)}) %collective-permute-start.6) | collective-permute-done | bytes 46112 | tf_op jit(solution)/shard_map/ppermute | solution.py:22
  55.0 5.2 %collective-permute-done.7 = f32[3,30,128]{1,2,0:T(8,128)S(1)} collective-permute-done((f32[3,30,128]{1,2,0:T(8,128)S(1)}, f32[3,30,128]{1,2,0:T(8,128)S(1)}, u32[]{:S(2)}, u32[]{:S(2)}) %collective-permute-start.7) | collective-permute-done | bytes 46112 | tf_op jit(solution)/shard_map/ppermute | solution.py:22
  60.2 1.7 gather_fusion.20
  62.0 1.7 gather_fusion.19
  63.8 1.7 gather_fusion.18
  81.5 3.2 %collective-permute-start.8 = (f32[3,30,128]{2,1,0:T(8,128)S(1)}, f32[3,30,128]{2,1,0:T(8,128)S(1)}, u32[]{:S(2)}, u32[]{:S(2)}) collective-permute-start(f32[3,30,128]{2,1,0:T(8,128)S(1)} %pad_maximum_fusion.16), channel_id=1, source_target_pairs={{1,0},{2,1},{3,2},{4,3},{5,4},{6,5},{7,6},{0,7},{9,8},{10,9},{11,1... | collective-permute-start | bytes 138248 | tf_op jit(solution)/shard_map/ppermute | solution.py:16
  84.7 1.7 collective-permute-done.8
  86.4 2.3 %collective-permute-start.10 = (f32[3,30,128]{2,1,0:T(8,128)S(1)}, f32[3,30,128]{2,1,0:T(8,128)S(1)}, u32[]{:S(2)}, u32[]{:S(2)}) collective-permute-start(f32[3,30,128]{2,1,0:T(8,128)S(1)} %pad_maximum_fusion.18), channel_id=1, source_target_pairs={{0,8},{8,16},{16,24},{1,9},{9,17},{17,25},{2,10},{10,18},{18,26},{... | collective-permute-start | bytes 138248 | tf_op jit(solution)/shard_map/ppermute | solution.py:22
  88.8 1.3 collective-permute-start.11
  90.5 4.2 %collective-permute-done.11 = f32[3,30,128]{2,1,0:T(8,128)S(1)} collective-permute-done((f32[3,30,128]{2,1,0:T(8,128)S(1)}, f32[3,30,128]{2,1,0:T(8,128)S(1)}, u32[]{:S(2)}, u32[]{:S(2)}) %collective-permute-start.11) | collective-permute-done | bytes 46112 | tf_op jit(solution)/shard_map/ppermute | solution.py:22
  95.1 2.9 %gather_fusion.30 = f32[960,30]{1,0:T(8,128)S(1)} fusion(f32[30,1664]{0,1:T(8,128)S(1)} %copy.932, s32[1024]{0:T(1024)S(1)} %pad_clamp_fusion.11), kind=kCustom, calls=%fused_computation.29.clone | custom fusion | bytes 234240 | tf_op jit(solution)/shard_map/jit(_take)/gather | solution.py:31
  98.0 2.9 %gather_fusion.29 = f32[960,30]{1,0:T(8,128)S(1)} fusion(f32[30,1664]{0,1:T(8,128)S(1)} %copy.932, s32[1024]{0:T(1024)S(1)} %pad_clamp_fusion.12), kind=kCustom, calls=%fused_computation.28.clone | custom fusion | bytes 234240 | tf_op jit(solution)/shard_map/jit(_take)/gather | solution.py:31
  111.4 3.1 %collective-permute-start.12 = (f32[3,30,128]{1,2,0:T(8,128)S(1)}, f32[3,30,128]{1,2,0:T(8,128)S(1)}, u32[]{:S(2)}, u32[]{:S(2)}) collective-permute-start(f32[3,30,128]{1,2,0:T(8,128)S(1)} %pad_maximum_fusion.4), channel_id=1, source_target_pairs={{1,0},{2,1},{3,2},{4,3},{5,4},{6,5},{7,6},{0,7},{9,8},{10,9},{11,1... | collective-permute-start | bytes 138248 | tf_op jit(solution)/shard_map/ppermute | solution.py:16
  114.6 3.0 %collective-permute-done.13 = f32[3,30,128]{1,2,0:T(8,128)S(1)} collective-permute-done((f32[3,30,128]{1,2,0:T(8,128)S(1)}, f32[3,30,128]{1,2,0:T(8,128)S(1)}, u32[]{:S(2)}, u32[]{:S(2)}) %collective-permute-start.13) | collective-permute-done | bytes 46112 | tf_op jit(solution)/shard_map/ppermute | solution.py:16
  117.7 2.8 %collective-permute-start.14 = (f32[3,30,128]{1,2,0:T(8,128)S(1)}, f32[3,30,128]{1,2,0:T(8,128)S(1)}, u32[]{:S(2)}, u32[]{:S(2)}) collective-permute-start(f32[3,30,128]{1,2,0:T(8,128)S(1)} %pad_maximum_fusion.6), channel_id=1, source_target_pairs={{0,8},{8,16},{16,24},{1,9},{9,17},{17,25},{2,10},{10,18},{18,26},{... | collective-permute-start | bytes 138248 | tf_op jit(solution)/shard_map/ppermute | solution.py:22
  120.6 1.5 collective-permute-start.15
  122.0 2.6 %collective-permute-done.14 = f32[3,30,128]{1,2,0:T(8,128)S(1)} collective-permute-done((f32[3,30,128]{1,2,0:T(8,128)S(1)}, f32[3,30,128]{1,2,0:T(8,128)S(1)}, u32[]{:S(2)}, u32[]{:S(2)}) %collective-permute-start.14) | collective-permute-done | bytes 46112 | tf_op jit(solution)/shard_map/ppermute | solution.py:22
  124.7 4.9 %collective-permute-done.15 = f32[3,30,128]{1,2,0:T(8,128)S(1)} collective-permute-done((f32[3,30,128]{1,2,0:T(8,128)S(1)}, f32[3,30,128]{1,2,0:T(8,128)S(1)}, u32[]{:S(2)}, u32[]{:S(2)}) %collective-permute-start.15) | collective-permute-done | bytes 46112 | tf_op jit(solution)/shard_map/ppermute | solution.py:22
  129.6 1.7 gather_fusion.41
  131.3 1.7 gather_fusion.40
  133.0 1.7 gather_fusion.39
  146.6 3.6 %collective-permute-start.16 = (f32[3,30,128]{2,1,0:T(8,128)S(1)}, f32[3,30,128]{2,1,0:T(8,128)S(1)}, u32[]{:S(2)}, u32[]{:S(2)}) collective-permute-start(f32[3,30,128]{2,1,0:T(8,128)S(1)} %pad_maximum_fusion.20), channel_id=1, source_target_pairs={{1,0},{2,1},{3,2},{4,3},{5,4},{6,5},{7,6},{0,7},{9,8},{10,9},{11,1... | collective-permute-start | bytes 138248 | tf_op jit(solution)/shard_map/ppermute | solution.py:16
  150.2 1.7 collective-permute-done.17
  152.0 2.3 %collective-permute-start.18 = (f32[3,30,128]{2,1,0:T(8,128)S(1)}, f32[3,30,128]{2,1,0:T(8,128)S(1)}, u32[]{:S(2)}, u32[]{:S(2)}) collective-permute-start(f32[3,30,128]{2,1,0:T(8,128)S(1)} %pad_maximum_fusion.22), channel_id=1, source_target_pairs={{0,8},{8,16},{16,24},{1,9},{9,17},{17,25},{2,10},{10,18},{18,26},{... | collective-permute-start | bytes 138248 | tf_op jit(solution)/shard_map/ppermute | solution.py:22
  154.3 1.3 collective-permute-start.19
  156.0 4.2 %collective-permute-done.19 = f32[3,30,128]{2,1,0:T(8,128)S(1)} collective-permute-done((f32[3,30,128]{2,1,0:T(8,128)S(1)}, f32[3,30,128]{2,1,0:T(8,128)S(1)}, u32[]{:S(2)}, u32[]{:S(2)}) %collective-permute-start.19) | collective-permute-done | bytes 46112 | tf_op jit(solution)/shard_map/ppermute | solution.py:22
  160.6 2.9 %gather_fusion.51 = f32[960,30]{1,0:T(8,128)S(1)} fusion(f32[30,1664]{0,1:T(8,128)S(1)} %copy.953, s32[1024]{0:T(1024)S(1)} %pad_clamp_fusion.11), kind=kCustom, calls=%fused_computation.31.clone | custom fusion | bytes 234240 | tf_op jit(solution)/shard_map/jit(_take)/gather | solution.py:31
  163.5 2.9 %gather_fusion.50 = f32[960,30]{1,0:T(8,128)S(1)} fusion(f32[30,1664]{0,1:T(8,128)S(1)} %copy.953, s32[1024]{0:T(1024)S(1)} %copy-done.8), kind=kCustom, calls=%fused_computation.30.clone | custom fusion | bytes 234240 | tf_op jit(solution)/shard_map/jit(_take)/gather | solution.py:31
  176.9 3.1 %collective-permute-start.20 = (f32[3,30,128]{1,2,0:T(8,128)S(1)}, f32[3,30,128]{1,2,0:T(8,128)S(1)}, u32[]{:S(2)}, u32[]{:S(2)}) collective-permute-start(f32[3,30,128]{1,2,0:T(8,128)S(1)} %pad_maximum_fusion.8), channel_id=1, source_target_pairs={{1,0},{2,1},{3,2},{4,3},{5,4},{6,5},{7,6},{0,7},{9,8},{10,9},{11,1... | collective-permute-start | bytes 138248 | tf_op jit(solution)/shard_map/ppermute | solution.py:16
  180.9 2.1 %collective-permute-done.21 = f32[3,30,128]{1,2,0:T(8,128)S(1)} collective-permute-done((f32[3,30,128]{1,2,0:T(8,128)S(1)}, f32[3,30,128]{1,2,0:T(8,128)S(1)}, u32[]{:S(2)}, u32[]{:S(2)}) %collective-permute-start.21) | collective-permute-done | bytes 46112 | tf_op jit(solution)/shard_map/ppermute | solution.py:16
  183.2 2.8 %collective-permute-start.22 = (f32[3,30,128]{1,2,0:T(8,128)S(1)}, f32[3,30,128]{1,2,0:T(8,128)S(1)}, u32[]{:S(2)}, u32[]{:S(2)}) collective-permute-start(f32[3,30,128]{1,2,0:T(8,128)S(1)} %pad_maximum_fusion.10), channel_id=1, source_target_pairs={{0,8},{8,16},{16,24},{1,9},{9,17},{17,25},{2,10},{10,18},{18,26},{... | collective-permute-start | bytes 138248 | tf_op jit(solution)/shard_map/ppermute | solution.py:22
  186.1 1.3 collective-permute-start.23
  187.4 1.8 collective-permute-done.22
  189.3 4.7 %collective-permute-done.23 = f32[3,30,128]{1,2,0:T(8,128)S(1)} collective-permute-done((f32[3,30,128]{1,2,0:T(8,128)S(1)}, f32[3,30,128]{1,2,0:T(8,128)S(1)}, u32[]{:S(2)}, u32[]{:S(2)}) %collective-permute-start.23) | collective-permute-done | bytes 46112 | tf_op jit(solution)/shard_map/ppermute | solution.py:22
  194.0 1.7 gather_fusion.62
  195.7 1.7 gather_fusion.61
  197.4 1.7 gather_fusion.60
  (700 shorter events, 75.4 us)
Async XLA Ops:
  1.8 5.2 %copy-start.173 = (pred[128]{0:T(512)(128)(4,1)}, pred[128]{0:T(512)(128)(4,1)S(1)}, u32[]{:S(2)}) copy-start(pred[128]{0:T(512)(128)(4,1)S(1)} %get-tuple-element.349) | copy-start | bytes 388
  1.8 15.0 %copy-start.175 = (pred[128]{0:T(512)(128)(4,1)}, pred[128]{0:T(512)(128)(4,1)S(1)}, u32[]{:S(2)}) copy-start(pred[128]{0:T(512)(128)(4,1)S(1)} %get-tuple-element.343) | copy-start | bytes 388
  1.8 15.0 %copy-start.168 = (pred[128]{0:T(512)(128)(4,1)}, pred[128]{0:T(512)(128)(4,1)S(1)}, u32[]{:S(2)}) copy-start(pred[128]{0:T(512)(128)(4,1)S(1)} %get-tuple-element.283) | copy-start | bytes 388
  4.1 14.0 %collective-permute-start.1 = (f32[3,30,128]{2,1,0:T(8,128)S(1)}, f32[3,30,128]{2,1,0:T(8,128)S(1)}, u32[]{:S(2)}, u32[]{:S(2)}) collective-permute-start(f32[3,30,128]{2,1,0:T(8,128)S(1)} %pad_maximum_fusion.13), channel_id=1, source_target_pairs={{7,0},{0,1},{1,2},{2,3},{3,4},{4,5},{5,6},{6,7},{15,8},{8,9},{9,10... | collective-permute-start | bytes 138248 | tf_op jit(solution)/shard_map/ppermute | solution.py:16
  7.0 11.1 %collective-permute-start = (f32[3,30,128]{2,1,0:T(8,128)S(1)}, f32[3,30,128]{2,1,0:T(8,128)S(1)}, u32[]{:S(2)}, u32[]{:S(2)}) collective-permute-start(f32[3,30,128]{2,1,0:T(8,128)S(1)} %pad_maximum_fusion.12), channel_id=1, source_target_pairs={{1,0},{2,1},{3,2},{4,3},{5,4},{6,5},{7,6},{0,7},{9,8},{10,9},{11,1... | collective-permute-start | bytes 138248 | tf_op jit(solution)/shard_map/ppermute | solution.py:16
  11.2 23.0 %copy-start.137 = (pred[960]{0:T(1024)(128)(4,1)}, pred[960]{0:T(1024)(128)(4,1)S(1)}, u32[]{:S(2)}) copy-start(pred[960]{0:T(1024)(128)(4,1)S(1)} %compare_and_fusion.3) | copy-start | bytes 2884
  11.9 22.3 %copy-start.140 = (pred[960]{0:T(1024)(128)(4,1)}, pred[960]{0:T(1024)(128)(4,1)S(1)}, u32[]{:S(2)}) copy-start(pred[960]{0:T(1024)(128)(4,1)S(1)} %compare_and_fusion.4) | copy-start | bytes 2884
  15.2 82.8 %copy-start.7 = (s32[1024]{0:T(1024)}, s32[1024]{0:T(1024)S(1)}, u32[]{:S(2)}) copy-start(s32[1024]{0:T(1024)S(1)} %pad_clamp_fusion.12) | copy-start | bytes 12292
  15.2 21.8 %copy-start.170 = (pred[128]{0:T(512)(128)(4,1)}, pred[128]{0:T(512)(128)(4,1)S(1)}, u32[]{:S(2)}) copy-start(pred[128]{0:T(512)(128)(4,1)S(1)} %get-tuple-element.337) | copy-start | bytes 388
  15.2 21.9 %copy-start.165 = (pred[128]{0:T(512)(128)(4,1)}, pred[128]{0:T(512)(128)(4,1)S(1)}, u32[]{:S(2)}) copy-start(pred[128]{0:T(512)(128)(4,1)S(1)} %get-tuple-element.325) | copy-start | bytes 388
  15.2 22.0 %copy-start.162 = (pred[128]{0:T(512)(128)(4,1)}, pred[128]{0:T(512)(128)(4,1)S(1)}, u32[]{:S(2)}) copy-start(pred[128]{0:T(512)(128)(4,1)S(1)} %get-tuple-element.327) | copy-start | bytes 388
  15.3 24.8 %copy-start.152 = (pred[128]{0:T(512)(128)(4,1)}, pred[128]{0:T(512)(128)(4,1)S(1)}, u32[]{:S(2)}) copy-start(pred[128]{0:T(512)(128)(4,1)S(1)} %get-tuple-element.331) | copy-start | bytes 388
  15.3 24.9 %copy-start.149 = (pred[128]{0:T(512)(128)(4,1)}, pred[128]{0:T(512)(128)(4,1)S(1)}, u32[]{:S(2)}) copy-start(pred[128]{0:T(512)(128)(4,1)S(1)} %get-tuple-element.333) | copy-start | bytes 388
  15.3 25.0 %copy-start.146 = (pred[128]{0:T(512)(128)(4,1)}, pred[128]{0:T(512)(128)(4,1)S(1)}, u32[]{:S(2)}) copy-start(pred[128]{0:T(512)(128)(4,1)S(1)} %get-tuple-element.335) | copy-start | bytes 388
  15.3 29.3 %copy-start.155 = (pred[128]{0:T(512)(128)(4,1)}, pred[128]{0:T(512)(128)(4,1)S(1)}, u32[]{:S(2)}) copy-start(pred[128]{0:T(512)(128)(4,1)S(1)} %get-tuple-element.329) | copy-start | bytes 388
  15.3 29.4 %copy-start.143 = (pred[128]{0:T(512)(128)(4,1)}, pred[128]{0:T(512)(128)(4,1)S(1)}, u32[]{:S(2)}) copy-start(pred[128]{0:T(512)(128)(4,1)S(1)} %get-tuple-element.265) | copy-start | bytes 388
  15.3 19.8 %copy-start.184 = (s32[1024]{0:T(1024)}, s32[1024]{0:T(1024)S(1)}, u32[]{:S(2)}) copy-start(s32[1024]{0:T(1024)S(1)} %pad_clamp_fusion.4) | copy-start | bytes 12292
  15.3 20.4 %copy-start.185 = (s32[1024]{0:T(1024)}, s32[1024]{0:T(1024)S(1)}, u32[]{:S(2)}) copy-start(s32[1024]{0:T(1024)S(1)} %pad_clamp_fusion.5) | copy-start | bytes 12292
  15.4 21.0 %copy-start.186 = (s32[1024]{0:T(1024)}, s32[1024]{0:T(1024)S(1)}, u32[]{:S(2)}) copy-start(s32[1024]{0:T(1024)S(1)} %pad_clamp_fusion.6) | copy-start | bytes 12292
  15.4 22.1 %copy-start.187 = (s32[1024]{0:T(1024)}, s32[1024]{0:T(1024)S(1)}, u32[]{:S(2)}) copy-start(s32[1024]{0:T(1024)S(1)} %pad_clamp_fusion.7) | copy-start | bytes 12292
  15.4 22.7 %copy-start.188 = (s32[1024]{0:T(1024)}, s32[1024]{0:T(1024)S(1)}, u32[]{:S(2)}) copy-start(s32[1024]{0:T(1024)S(1)} %pad_clamp_fusion.8) | copy-start | bytes 12292
  15.4 23.3 %copy-start.189 = (s32[1024]{0:T(1024)}, s32[1024]{0:T(1024)S(1)}, u32[]{:S(2)}) copy-start(s32[1024]{0:T(1024)S(1)} %pad_clamp_fusion.9) | copy-start | bytes 12292
  15.5 23.9 %copy-start.190 = (s32[1024]{0:T(1024)}, s32[1024]{0:T(1024)S(1)}, u32[]{:S(2)}) copy-start(s32[1024]{0:T(1024)S(1)} %pad_clamp_fusion.10) | copy-start | bytes 12292
  15.5 28.5 %copy-start.191 = (s32[1024]{0:T(1024)}, s32[1024]{0:T(1024)S(1)}, u32[]{:S(2)}) copy-start(s32[1024]{0:T(1024)S(1)} %pad_clamp_fusion.3) | copy-start | bytes 12292
  16.2 115.1 %copy-start.3 = (s32[1024]{0:T(1024)}, s32[1024]{0:T(1024)S(1)}, u32[]{:S(2)}) copy-start(s32[1024]{0:T(1024)S(1)} %pad_clamp_fusion.1) | copy-start | bytes 12292
  16.9 116.1 %copy-start.5 = (s32[1024]{0:T(1024)}, s32[1024]{0:T(1024)S(1)}, u32[]{:S(2)}) copy-start(s32[1024]{0:T(1024)S(1)} %pad_clamp_fusion.2) | copy-start | bytes 12292
  18.2 5.6 %collective-permute-start.2 = (f32[3,30,128]{2,1,0:T(8,128)S(1)}, f32[3,30,128]{2,1,0:T(8,128)S(1)}, u32[]{:S(2)}, u32[]{:S(2)}) collective-permute-start(f32[3,30,128]{2,1,0:T(8,128)S(1)} %pad_maximum_fusion.14), channel_id=1, source_target_pairs={{0,8},{8,16},{16,24},{1,9},{9,17},{17,25},{2,10},{10,18},{18,26},{... | collective-permute-start | bytes 138248 | tf_op jit(solution)/shard_map/ppermute | solution.py:22
  22.1 6.0 %collective-permute-start.3 = (f32[3,30,128]{2,1,0:T(8,128)S(1)}, f32[3,30,128]{2,1,0:T(8,128)S(1)}, u32[]{:S(2)}, u32[]{:S(2)}) collective-permute-start(f32[3,30,128]{2,1,0:T(8,128)S(1)} %pad_maximum_fusion.15), channel_id=1, source_target_pairs={{8,0},{16,8},{24,16},{9,1},{17,9},{25,17},{10,2},{18,10},{26,18},{... | collective-permute-start | bytes 138248 | tf_op jit(solution)/shard_map/ppermute | solution.py:22
  37.4 7.4 %collective-permute-start.5 = (f32[3,30,128]{1,2,0:T(8,128)S(1)}, f32[3,30,128]{1,2,0:T(8,128)S(1)}, u32[]{:S(2)}, u32[]{:S(2)}) collective-permute-start(f32[3,30,128]{1,2,0:T(8,128)S(1)} %pad_maximum_fusion.1), channel_id=1, source_target_pairs={{7,0},{0,1},{1,2},{2,3},{3,4},{4,5},{5,6},{6,7},{15,8},{8,9},{9,10... | collective-permute-start | bytes 138248 | tf_op jit(solution)/shard_map/ppermute | solution.py:16
  40.4 6.8 %collective-permute-start.4 = (f32[3,30,128]{1,2,0:T(8,128)S(1)}, f32[3,30,128]{1,2,0:T(8,128)S(1)}, u32[]{:S(2)}, u32[]{:S(2)}) collective-permute-start(f32[3,30,128]{1,2,0:T(8,128)S(1)} %pad_maximum_fusion), channel_id=1, source_target_pairs={{1,0},{2,1},{3,2},{4,3},{5,4},{6,5},{7,6},{0,7},{9,8},{10,9},{11,1... | collective-permute-start | bytes 138248 | tf_op jit(solution)/shard_map/ppermute | solution.py:16
  47.2 7.7 %collective-permute-start.6 = (f32[3,30,128]{1,2,0:T(8,128)S(1)}, f32[3,30,128]{1,2,0:T(8,128)S(1)}, u32[]{:S(2)}, u32[]{:S(2)}) collective-permute-start(f32[3,30,128]{1,2,0:T(8,128)S(1)} %pad_maximum_fusion.2), channel_id=1, source_target_pairs={{0,8},{8,16},{16,24},{1,9},{9,17},{17,25},{2,10},{10,18},{18,26},{... | collective-permute-start | bytes 138248 | tf_op jit(solution)/shard_map/ppermute | solution.py:22
  51.5 8.6 %collective-permute-start.7 = (f32[3,30,128]{1,2,0:T(8,128)S(1)}, f32[3,30,128]{1,2,0:T(8,128)S(1)}, u32[]{:S(2)}, u32[]{:S(2)}) collective-permute-start(f32[3,30,128]{1,2,0:T(8,128)S(1)} %pad_maximum_fusion.3), channel_id=1, source_target_pairs={{8,0},{16,8},{24,16},{9,1},{17,9},{25,17},{10,2},{18,10},{26,18},{... | collective-permute-start | bytes 138248 | tf_op jit(solution)/shard_map/ppermute | solution.py:22
  78.3 6.4 %collective-permute-start.9 = (f32[3,30,128]{2,1,0:T(8,128)S(1)}, f32[3,30,128]{2,1,0:T(8,128)S(1)}, u32[]{:S(2)}, u32[]{:S(2)}) collective-permute-start(f32[3,30,128]{2,1,0:T(8,128)S(1)} %pad_maximum_fusion.17), channel_id=1, source_target_pairs={{7,0},{0,1},{1,2},{2,3},{3,4},{4,5},{5,6},{6,7},{15,8},{8,9},{9,10... | collective-permute-start | bytes 138248 | tf_op jit(solution)/shard_map/ppermute | solution.py:16
  81.5 4.9 %collective-permute-start.8 = (f32[3,30,128]{2,1,0:T(8,128)S(1)}, f32[3,30,128]{2,1,0:T(8,128)S(1)}, u32[]{:S(2)}, u32[]{:S(2)}) collective-permute-start(f32[3,30,128]{2,1,0:T(8,128)S(1)} %pad_maximum_fusion.16), channel_id=1, source_target_pairs={{1,0},{2,1},{3,2},{4,3},{5,4},{6,5},{7,6},{0,7},{9,8},{10,9},{11,1... | collective-permute-start | bytes 138248 | tf_op jit(solution)/shard_map/ppermute | solution.py:16
  86.4 4.0 %collective-permute-start.10 = (f32[3,30,128]{2,1,0:T(8,128)S(1)}, f32[3,30,128]{2,1,0:T(8,128)S(1)}, u32[]{:S(2)}, u32[]{:S(2)}) collective-permute-start(f32[3,30,128]{2,1,0:T(8,128)S(1)} %pad_maximum_fusion.18), channel_id=1, source_target_pairs={{0,8},{8,16},{16,24},{1,9},{9,17},{17,25},{2,10},{10,18},{18,26},{... | collective-permute-start | bytes 138248 | tf_op jit(solution)/shard_map/ppermute | solution.py:22
  88.8 6.0 %collective-permute-start.11 = (f32[3,30,128]{2,1,0:T(8,128)S(1)}, f32[3,30,128]{2,1,0:T(8,128)S(1)}, u32[]{:S(2)}, u32[]{:S(2)}) collective-permute-start(f32[3,30,128]{2,1,0:T(8,128)S(1)} %pad_maximum_fusion.19), channel_id=1, source_target_pairs={{8,0},{16,8},{24,16},{9,1},{17,9},{25,17},{10,2},{18,10},{26,18},{... | collective-permute-start | bytes 138248 | tf_op jit(solution)/shard_map/ppermute | solution.py:22
  109.3 8.2 %collective-permute-start.13 = (f32[3,30,128]{1,2,0:T(8,128)S(1)}, f32[3,30,128]{1,2,0:T(8,128)S(1)}, u32[]{:S(2)}, u32[]{:S(2)}) collective-permute-start(f32[3,30,128]{1,2,0:T(8,128)S(1)} %pad_maximum_fusion.5), channel_id=1, source_target_pairs={{7,0},{0,1},{1,2},{2,3},{3,4},{4,5},{5,6},{6,7},{15,8},{8,9},{9,10... | collective-permute-start | bytes 138248 | tf_op jit(solution)/shard_map/ppermute | solution.py:16
  111.4 6.3 %collective-permute-start.12 = (f32[3,30,128]{1,2,0:T(8,128)S(1)}, f32[3,30,128]{1,2,0:T(8,128)S(1)}, u32[]{:S(2)}, u32[]{:S(2)}) collective-permute-start(f32[3,30,128]{1,2,0:T(8,128)S(1)} %pad_maximum_fusion.4), channel_id=1, source_target_pairs={{1,0},{2,1},{3,2},{4,3},{5,4},{6,5},{7,6},{0,7},{9,8},{10,9},{11,1... | collective-permute-start | bytes 138248 | tf_op jit(solution)/shard_map/ppermute | solution.py:16
  117.7 6.9 %collective-permute-start.14 = (f32[3,30,128]{1,2,0:T(8,128)S(1)}, f32[3,30,128]{1,2,0:T(8,128)S(1)}, u32[]{:S(2)}, u32[]{:S(2)}) collective-permute-start(f32[3,30,128]{1,2,0:T(8,128)S(1)} %pad_maximum_fusion.6), channel_id=1, source_target_pairs={{0,8},{8,16},{16,24},{1,9},{9,17},{17,25},{2,10},{10,18},{18,26},{... | collective-permute-start | bytes 138248 | tf_op jit(solution)/shard_map/ppermute | solution.py:22
  120.6 9.0 %collective-permute-start.15 = (f32[3,30,128]{1,2,0:T(8,128)S(1)}, f32[3,30,128]{1,2,0:T(8,128)S(1)}, u32[]{:S(2)}, u32[]{:S(2)}) collective-permute-start(f32[3,30,128]{1,2,0:T(8,128)S(1)} %pad_maximum_fusion.7), channel_id=1, source_target_pairs={{8,0},{16,8},{24,16},{9,1},{17,9},{25,17},{10,2},{18,10},{26,18},{... | collective-permute-start | bytes 138248 | tf_op jit(solution)/shard_map/ppermute | solution.py:22
  146.1 5.8 %collective-permute-start.17 = (f32[3,30,128]{2,1,0:T(8,128)S(1)}, f32[3,30,128]{2,1,0:T(8,128)S(1)}, u32[]{:S(2)}, u32[]{:S(2)}) collective-permute-start(f32[3,30,128]{2,1,0:T(8,128)S(1)} %pad_maximum_fusion.21), channel_id=1, source_target_pairs={{7,0},{0,1},{1,2},{2,3},{3,4},{4,5},{5,6},{6,7},{15,8},{8,9},{9,10... | collective-permute-start | bytes 138248 | tf_op jit(solution)/shard_map/ppermute | solution.py:16
  146.6 5.3 %collective-permute-start.16 = (f32[3,30,128]{2,1,0:T(8,128)S(1)}, f32[3,30,128]{2,1,0:T(8,128)S(1)}, u32[]{:S(2)}, u32[]{:S(2)}) collective-permute-start(f32[3,30,128]{2,1,0:T(8,128)S(1)} %pad_maximum_fusion.20), channel_id=1, source_target_pairs={{1,0},{2,1},{3,2},{4,3},{5,4},{6,5},{7,6},{0,7},{9,8},{10,9},{11,1... | collective-permute-start | bytes 138248 | tf_op jit(solution)/shard_map/ppermute | solution.py:16
  152.0 4.0 %collective-permute-start.18 = (f32[3,30,128]{2,1,0:T(8,128)S(1)}, f32[3,30,128]{2,1,0:T(8,128)S(1)}, u32[]{:S(2)}, u32[]{:S(2)}) collective-permute-start(f32[3,30,128]{2,1,0:T(8,128)S(1)} %pad_maximum_fusion.22), channel_id=1, source_target_pairs={{0,8},{8,16},{16,24},{1,9},{9,17},{17,25},{2,10},{10,18},{18,26},{... | collective-permute-start | bytes 138248 | tf_op jit(solution)/shard_map/ppermute | solution.py:22
  154.3 6.0 %collective-permute-start.19 = (f32[3,30,128]{2,1,0:T(8,128)S(1)}, f32[3,30,128]{2,1,0:T(8,128)S(1)}, u32[]{:S(2)}, u32[]{:S(2)}) collective-permute-start(f32[3,30,128]{2,1,0:T(8,128)S(1)} %pad_maximum_fusion.23), channel_id=1, source_target_pairs={{8,0},{16,8},{24,16},{9,1},{17,9},{25,17},{10,2},{18,10},{26,18},{... | collective-permute-start | bytes 138248 | tf_op jit(solution)/shard_map/ppermute | solution.py:22
  174.8 8.2 %collective-permute-start.21 = (f32[3,30,128]{1,2,0:T(8,128)S(1)}, f32[3,30,128]{1,2,0:T(8,128)S(1)}, u32[]{:S(2)}, u32[]{:S(2)}) collective-permute-start(f32[3,30,128]{1,2,0:T(8,128)S(1)} %pad_maximum_fusion.9), channel_id=1, source_target_pairs={{7,0},{0,1},{1,2},{2,3},{3,4},{4,5},{5,6},{6,7},{15,8},{8,9},{9,10... | collective-permute-start | bytes 138248 | tf_op jit(solution)/shard_map/ppermute | solution.py:16
  176.9 6.3 %collective-permute-start.20 = (f32[3,30,128]{1,2,0:T(8,128)S(1)}, f32[3,30,128]{1,2,0:T(8,128)S(1)}, u32[]{:S(2)}, u32[]{:S(2)}) collective-permute-start(f32[3,30,128]{1,2,0:T(8,128)S(1)} %pad_maximum_fusion.8), channel_id=1, source_target_pairs={{1,0},{2,1},{3,2},{4,3},{5,4},{6,5},{7,6},{0,7},{9,8},{10,9},{11,1... | collective-permute-start | bytes 138248 | tf_op jit(solution)/shard_map/ppermute | solution.py:16
  183.2 6.0 %collective-permute-start.22 = (f32[3,30,128]{1,2,0:T(8,128)S(1)}, f32[3,30,128]{1,2,0:T(8,128)S(1)}, u32[]{:S(2)}, u32[]{:S(2)}) collective-permute-start(f32[3,30,128]{1,2,0:T(8,128)S(1)} %pad_maximum_fusion.10), channel_id=1, source_target_pairs={{0,8},{8,16},{16,24},{1,9},{9,17},{17,25},{2,10},{10,18},{18,26},{... | collective-permute-start | bytes 138248 | tf_op jit(solution)/shard_map/ppermute | solution.py:22
  186.1 7.9 %collective-permute-start.23 = (f32[3,30,128]{1,2,0:T(8,128)S(1)}, f32[3,30,128]{1,2,0:T(8,128)S(1)}, u32[]{:S(2)}, u32[]{:S(2)}) collective-permute-start(f32[3,30,128]{1,2,0:T(8,128)S(1)} %pad_maximum_fusion.11), channel_id=1, source_target_pairs={{8,0},{16,8},{24,16},{9,1},{17,9},{25,17},{10,2},{18,10},{26,18},{... | collective-permute-start | bytes 138248 | tf_op jit(solution)/shard_map/ppermute | solution.py:22
  (181 other events, 224.8 us)
where the time goes:
time: 206 us; the launch traced here: 205 us
  local copies, waits for them, and re-layouts  92.4 us (45%)
  starting transfers between devices  47.8 us (23%)
  waiting for transfers between devices  46.5 us (23%)
  other arithmetic  13.8 us (7%)
  between operations  4.19 us (2%)
    gather x72, local copies, waits for them, and re-layouts, extend(): jnp.take(source, send_list[member], axis=1)  36.5 us
    ppermute x12, waiting for transfers between devices, passed_along(): lax.ppermute(value, axis, [(source, source + steps) for source in range(f...  35.3 us
    ppermute x12, starting transfers between devices, passed_along(): lax.ppermute(value, axis, [(source, source + steps) for source in range(f...  26.4 us
    ppermute x12, starting transfers between devices, from_behind(): return lax.ppermute(block, axis, route)  21.4 us
    unnamed x459, local copies, waits for them, and re-layouts  19.8 us
    ppermute x12, waiting for transfers between devices, from_behind(): return lax.ppermute(block, axis, route)  11.1 us
    gather x3, local copies, waits for them, and re-layouts, edge_update(): jnp.take(extended, edge_cells[1], axis=1)  8.64 us
    gather x3, local copies, waits for them, and re-layouts, edge_update(): jnp.take(extended, edge_cells[0], axis=1)  8.64 us
  transfers between devices with their start and end apart: 24, of which 20 were waited for; matrix products, arithmetic and copies ran while one was open for 7% of the time, Pallas kernels for 0%

commit v1 on v0

v1 whole, which is shorter than its diff:
```python
import jax
import jax.numpy as jnp
from jax import lax
from jax.experimental import pallas as pl
from jax.experimental.pallas import tpu as pltpu
from jax.sharding import PartitionSpec as P

NSUB = 3
OFFSETS = ((-1, -1), (-1, 0), (-1, 1), (0, -1), (0, 1), (1, -1), (1, 0), (1, 1))
ORDER = (3, 4, 1, 6, 0, 2, 5, 7)
GROUPS = ((0, 2), (2, 8))
SEND_ORDER = (0, 2, 5, 7, 1, 6, 3, 4)
step_scale = 0.5
MESH = pl.DeviceIdType.MESH
F32, BF16 = jnp.float32, jnp.bfloat16


def split(x):
    hi = x.astype(BF16)
    lo = (x - hi.astype(F32)).astype(BF16)
    return jnp.concatenate([hi, lo], axis=0)


def joined(y):
    half = y.shape[0] // 2
    return y[:half] + y[half:]


def dot(x, w):
    return jnp.dot(x, w, preferred_element_type=F32)


def round_up(n, m):
    return (n + m - 1) // m * m


def build(dst, row0, rows, lane0, plus, minus, base):
    chunk = 32
    width = plus.shape[1]

    def body(i, carry):
        key = lax.broadcasted_iota(jnp.int32, (chunk, width), 0) + (base + i * chunk)
        hot = jnp.where(key == plus, 1.0, 0.0)
        if minus is not None:
            hot = hot - jnp.where(key == minus, 1.0, 0.0)
        start = pl.multiple_of(row0 + i * chunk, chunk)
        dst[pl.ds(start, chunk), lane0 : lane0 + width] = hot.astype(BF16)
        return carry

    lax.fori_loop(0, rows // chunk, body, 0)


def kernel(
    n_lat, n_lon, nlev, cells, edges, halo,
    p_in, v_in, ec, ce, sc, se, inv_dual, weight, sound, coupling,
    p_out, v_out,
    pf, vf, s_cells, s_edges, a_mat, b_mat, p_send, v_send, p_halo, v_halo,
    t_inv, t_low, t_up, work,
    p_ss, p_rs, v_ss, v_rs,
):
    a, b = lax.axis_index("lat"), lax.axis_index("lon")
    ecols = vf.shape[1]
    below, above = a > 0, a < n_lat - 1

    def if_there(p, fn):
        if p == 0:
            fn()
        else:
            pl.when(below if p < 0 else above)(fn)

    def target(offset):
        return (a + offset[0], lax.rem(b + offset[1] + n_lon, n_lon))

    p_halo[...] = jnp.zeros_like(p_halo)
    v_halo[...] = jnp.zeros_like(v_halo)

    barrier = pltpu.get_barrier_semaphore()
    for lat_step in (0, -1, 1):
        def greet(lat_step=lat_step):
            for offset in OFFSETS:
                if offset[0] == lat_step:
                    pl.semaphore_signal(
                        barrier, inc=1, device_id=target(offset), device_id_type=MESH
                    )
        if_there(lat_step, greet)

    pf[nlev - nlev % 8 :, :] = jnp.zeros_like(pf[nlev - nlev % 8 :, :])
    pf[0:nlev, :] = p_in[0]
    vf[...] = jnp.zeros_like(vf)
    vf[0:nlev, 0:edges] = v_in[0]
    for member in range(8):
        build(s_cells, 0, cells, member * halo, sc[0, member : member + 1, :], None, 0)

    bands = (a + n_lat - 1) // n_lat + (2 * n_lat - 2 - a) // n_lat
    pl.semaphore_wait(barrier, 2 + 3 * bands)

    def copy(member, send, land, ss, rs):
        spot = ORDER.index(7 - member)
        return pltpu.make_async_remote_copy(
            src_ref=send.at[member], dst_ref=land.at[spot],
            send_sem=ss.at[member], recv_sem=rs.at[spot],
            device_id=target(OFFSETS[member]), device_id_type=MESH,
        )

    def launch(source, selector, send, land, ss, rs):
        pieces = joined(dot(source, selector[...]))
        for member in range(8):
            send[member] = pieces[:, member * halo : (member + 1) * halo]
        for member in SEND_ORDER:
            if_there(OFFSETS[member][0], lambda: copy(member, send, land, ss, rs).start())

    def arrive(lo, hi, send, land, ss, rs):
        for spot in range(lo, hi):
            slot = ORDER[spot]
            if_there(OFFSETS[slot][0], lambda: copy(7 - slot, send, land, ss, rs).wait_recv())
        return split(jnp.concatenate([land[spot] for spot in range(lo, hi)], axis=1))

    def retire(send, land, ss, rs):
        for member in range(8):
            if_there(OFFSETS[member][0], lambda: copy(member, send, land, ss, rs).wait_send())

    for substep in range(NSUB):
        source = split(pf[...])
        launch(source, s_cells, p_send, p_halo, p_ss, p_rs)
        if substep == 0:
            first, second = ec[0, 0:1, :], ec[0, 1:2, :]
            build(a_mat, 0, cells, 0, second, first, 0)
            for spot, slot in enumerate(ORDER):
                build(a_mat, cells + spot * halo, halo, 0, second, first, cells + slot * halo)
            for member in range(8):
                build(s_edges, 0, ecols, member * halo, se[0, member : member + 1, :], None, 0)
        gradient = dot(source, a_mat[0:cells, :])
        for lo, hi in GROUPS:
            got = arrive(lo, hi, p_send, p_halo, p_ss, p_rs)
            gradient += dot(got, a_mat[cells + lo * halo : cells + hi * halo, :])
        retire(p_send, p_halo, p_ss, p_rs)
        vf[:, 0:edges] = vf[:, 0:edges] - (step_scale * inv_dual[...]) * joined(gradient)

        source = split(vf[...])
        launch(source, s_edges, v_send, v_halo, v_ss, v_rs)
        if substep == 0:
            for j in range(3):
                wanted = ce[0, j : j + 1, :]
                build(b_mat, 0, ecols, j * cells, wanted, None, 0)
                for spot, slot in enumerate(ORDER):
                    build(b_mat, ecols + spot * halo, halo, j * cells, wanted, None, edges + slot * halo)
            ratio = inverse = None
            for level in range(nlev):
                here = coupling[0, level : level + 1, :]
                if level == 0:
                    divisor = 1.0 + here
                else:
                    lower = coupling[0, level - 1 : level, :]
                    divisor = 1.0 + lower + here + lower * ratio
                inverse = 1.0 / divisor
                ratio = -here * inverse
                t_inv[level : level + 1, :] = inverse
                t_up[level : level + 1, :] = ratio
                if level > 0:
                    t_low[level : level + 1, :] = lower * inverse
        taken = dot(source, b_mat[0:ecols, :])
        for lo, hi in GROUPS:
            got = arrive(lo, hi, v_send, v_halo, v_ss, v_rs)
            taken += dot(got, b_mat[ecols + lo * halo : ecols + hi * halo, :])
        retire(v_send, v_halo, v_ss, v_rs)
        taken = joined(taken)
        divergence = taken[:, 0:cells] * weight[0, 0:1, :]
        for j in (1, 2):
            divergence += taken[:, j * cells : (j + 1) * cells] * weight[0, j : j + 1, :]
        right = pf[...] - sound[...] * divergence
        work[0:nlev, :] = right[0:nlev] * t_inv[...]

        current = work[0:1, :]
        for level in range(1, nlev):
            current = work[level : level + 1, :] + t_low[level : level + 1, :] * current
            work[level : level + 1, :] = current
        pf[nlev - 1 : nlev, :] = current
        for level in range(nlev - 2, -1, -1):
            current = work[level : level + 1, :] - t_up[level : level + 1, :] * current
            pf[level : level + 1, :] = current

    p_out[0] = pf[0:nlev, :]
    v_out[0] = vf[0:nlev, 0:edges]


def on_device(*args):
    pressure, velocity, send_cells = args[0], args[1], args[4]
    n_lat, n_lon = lax.axis_size("lat"), lax.axis_size("lon")
    nlev, cells, edges = pressure.shape[1], pressure.shape[2], velocity.shape[2]
    halo = send_cells.shape[2]
    rows, ecols = round_up(nlev, 32), round_up(edges, 128)
    vmem = pl.BlockSpec(memory_space=pltpu.VMEM)
    dma8 = pltpu.SemaphoreType.DMA((8,))

    def body(*refs):
        kernel(n_lat, n_lon, nlev, cells, edges, halo, *refs)

    return tuple(pl.pallas_call(
        body,
        name="substeps",
        out_shape=(
            jax.ShapeDtypeStruct(pressure.shape, F32),
            jax.ShapeDtypeStruct(velocity.shape, F32),
        ),
        in_specs=[vmem] * len(args),
        out_specs=(vmem, vmem),
        scratch_shapes=[
            pltpu.VMEM((rows, cells), F32),
            pltpu.VMEM((rows, ecols), F32),
            pltpu.VMEM((cells, 8 * halo), BF16),
            pltpu.VMEM((ecols, 8 * halo), BF16),
            pltpu.VMEM((cells + 8 * halo, edges), BF16),
            pltpu.VMEM((ecols + 8 * halo, 3 * cells), BF16),
            pltpu.VMEM((8, rows, halo), F32),
            pltpu.VMEM((8, rows, halo), F32),
            pltpu.VMEM((8, rows, halo), F32),
            pltpu.VMEM((8, rows, halo), F32),
            pltpu.VMEM((nlev, cells), F32),
            pltpu.VMEM((nlev, cells), F32),
            pltpu.VMEM((nlev, cells), F32),
            pltpu.VMEM((rows, cells), F32),
            dma8, dma8, dma8, dma8,
        ],
        compiler_params=pltpu.CompilerParams(collective_id=0, has_side_effects=True, vmem_limit_bytes=40 * 1024 * 1024),
    )(*args))


def solution(mesh):
    band = P("lat", None, "lon")
    flat = P("lat", "lon")
    return jax.shard_map(
        on_device,
        mesh=mesh,
        in_specs=(band, band, band, band, band, band, flat, band, flat, band),
        out_specs=(band, band),
        check_vma=False,
    )
```

time: 206 us -> 43.7 us (0.21)
  local copies, waits for them, and re-layouts: 92.4 us -> 3.85 us
  starting transfers between devices: 47.8 us -> 0 us
  waiting for transfers between devices: 46.5 us -> 0 us
  Pallas kernels: 0 us -> 38.8 us
  other arithmetic: 13.8 us -> 0 us
  between operations: 4.19 us -> 0.73 us
    gather x96 -> x0, local copies, waits for them, and re-layouts: 70.1 us -> none  [the longest x72 36.5 us: extend(): jnp.take(source, send_list[member], axis=1)]
    ppermute x24 -> x0, starting transfers between devices: 47.8 us -> none  [the longest x12 26.4 us: passed_along(): lax.ppermute(value, axis, [(source, source + steps) for source in range(f...]
    ppermute x24 -> x0, waiting for transfers between devices: 46.5 us -> none  [the longest x12 35.3 us: passed_along(): lax.ppermute(value, axis, [(source, source + steps) for source in range(f...]
    pallas_call x0 -> x1, Pallas kernels: none -> 38.8 us  [on_device(): pl.pallas_call(body, name='substeps', out_shape=(jax.ShapeDtypeStruct(pre...]
    unnamed x459 -> x21, local copies, waits for them, and re-layouts: 19.8 us -> 2.36 us
    sub x6 -> x0, other arithmetic: 3.21 us -> none  [the longest x3 2.42 us: column_solve(): result.insert(0, scaled[level_index] - ratios[level_index] * result[0])]
    unnamed x4 -> x0, other arithmetic: 3.21 us -> none
    div x3 -> x0, other arithmetic: 3.01 us -> none  [column_solve(): current = (right_side[level_index] - lower_term * scaled[-1]) / divisor]
  transfers between devices with their start and end apart: 24 -> 0, of which waited for: 20 -> 0; matrix products, arithmetic and copies ran while one was open for 7% -> 0% of each run, Pallas kernels for 0% -> 0%
where the time goes in v1:
time: 43.7 us; the launch traced here: 43.4 us
  Pallas kernels  38.8 us (89%)
  local copies, waits for them, and re-layouts  3.85 us (9%)
  between operations  0.73 us (2%)
    pallas_call x1, Pallas kernels, on_device(): pl.pallas_call(body, name='substeps', out_shape=(jax.ShapeDtypeStruct(pre...  38.8 us
    unnamed x21, local copies, waits for them, and re-layouts  2.36 us
    pallas_call x2, local copies, waits for them, and re-layouts, on_device(): pl.pallas_call(body, name='substeps', out_shape=(jax.ShapeDtypeStruct(pre...  1.49 us

profile of v1, /device:TPU:0, one launch (start us, length us, event | category | flops | bytes accessed | tf_op | source)
XLA Modules:
  0.0 43.4 jit_solution(10192782898564839432)
XLA Ops:
  0.6 0.0 copy-start.7
  0.6 0.7 %copy.14.refs_3_ = s32[1,3,640]{2,1,0:T(4,128)S(1)} copy(s32[1,3,640]{2,0,1:T(1,128)} %param.13) | data formatting | bytes 15360 | tf_op args[3]
  1.3 0.0 copy-done.7
  1.3 0.0 copy-start.6
  1.4 0.0 copy-start.5
  1.4 0.9 %copy.12.refs_0_ = f32[1,30,640]{2,1,0:T(8,128)S(1)} copy(f32[1,30,640]{2,0,1:T(1,128)} %param.10) | data formatting | bytes 153600 | tf_op args[0]
  2.3 0.0 copy-done.6
  2.3 0.0 copy-done.5
  2.3 0.0 copy-start
  2.3 0.0 copy-start.1
  2.4 0.0 copy-start.2
  2.4 0.0 copy-start.3
  2.4 0.0 copy-start.4
  2.4 0.6 %copy-done = s32[1,2,960]{2,1,0:T(2,128)S(1)} copy-done((s32[1,2,960]{2,1,0:T(2,128)S(1)}, s32[1,2,960]{2,1,0:T(2,128)}, u32[]{:S(2)}) %copy-start) | copy-done | bytes 7704
  3.0 0.0 copy-done.1
  3.0 0.0 copy-done.2
  3.1 0.0 copy-done.3
  3.1 0.0 copy-done.4
  3.1 38.8 %substeps.1 = (f32[1,30,640]{2,1,0:T(8,128)S(1)}, f32[1,30,960]{2,1,0:T(8,128)S(1)}) custom-call(f32[1,30,640]{2,1,0:T(8,128)S(1)} %copy.12.refs_0_, f32[1,30,960]{2,1,0:T(8,128)S(1)} %copy.13.refs_1_, s32[1,2,960]{2,1,0:T(2,128)S(1)} %copy-done, s32[1,3,640]{2,1,0:T(4,128)S(1)} %copy.14.refs_3_, s32[1,8,128]{2,1,0:T(8,128)S(1)} %copy-done.1, ...), custom_call_target="tpu_custom_call" | custom-call | tf_op jit(solution)/shard_map/substeps/pallas_call | solution.py:198
  41.9 0.7 %copy.17 = f32[1,30,640]{2,0,1:T(1,128)} copy(f32[1,30,640]{2,1,0:T(8,128)S(1)} %get-tuple-element.2) | data formatting | bytes 153600 | tf_op jit(solution)/shard_map/substeps/pallas_call | solution.py:198
  42.6 0.8 %copy.18 = f32[1,30,960]{2,0,1:T(1,128)} copy(f32[1,30,960]{2,1,0:T(8,128)S(1)} %get-tuple-element.3) | data formatting | bytes 230400 | tf_op jit(solution)/shard_map/substeps/pallas_call | solution.py:198
  (3 shorter events, 0.0 us)
Async XLA Ops:
  0.6 0.7 %copy-start.7 = (f32[1,3,640]{2,0,1:T(1,128)S(1)}, f32[1,3,640]{2,0,1:T(1,128)}, u32[]{:S(2)}) copy-start(f32[1,3,640]{2,0,1:T(1,128)} %param.17) | copy-start | bytes 23044
  1.3 1.0 %copy-start.6 = (f32[1,30,640]{2,0,1:T(1,128)S(1)}, f32[1,30,640]{2,0,1:T(1,128)}, u32[]{:S(2)}) copy-start(f32[1,30,640]{2,0,1:T(1,128)} %param.19) | copy-start | bytes 230404
  1.4 1.0 %copy-start.5 = (f32[1,30,960]{2,0,1:T(1,128)S(1)}, f32[1,30,960]{2,0,1:T(1,128)}, u32[]{:S(2)}) copy-start(f32[1,30,960]{2,0,1:T(1,128)} %param.11) | copy-start | bytes 345604
  2.3 0.7 %copy-start = (s32[1,2,960]{2,1,0:T(2,128)S(1)}, s32[1,2,960]{2,1,0:T(2,128)}, u32[]{:S(2)}) copy-start(s32[1,2,960]{2,1,0:T(2,128)} %refs_2_.1) | copy-start | bytes 23044
  2.3 0.7 %copy-start.1 = (s32[1,8,128]{2,1,0:T(8,128)S(1)}, s32[1,8,128]{2,1,0:T(8,128)}, u32[]{:S(2)}) copy-start(s32[1,8,128]{2,1,0:T(8,128)} %refs_4_.1) | copy-start | bytes 12292
  2.4 0.7 %copy-start.2 = (s32[1,8,128]{2,1,0:T(8,128)S(1)}, s32[1,8,128]{2,1,0:T(8,128)}, u32[]{:S(2)}) copy-start(s32[1,8,128]{2,1,0:T(8,128)} %refs_5_.1) | copy-start | bytes 12292
  2.4 0.7 %copy-start.3 = (f32[1,960]{1,0:T(1,128)S(1)}, f32[1,960]{1,0:T(1,128)}, u32[]{:S(2)}) copy-start(f32[1,960]{1,0:T(1,128)} %refs_6_.1) | copy-start | bytes 11524
  2.4 0.7 %copy-start.4 = (f32[1,640]{1,0:T(1,128)S(1)}, f32[1,640]{1,0:T(1,128)}, u32[]{:S(2)}) copy-start(f32[1,640]{1,0:T(1,128)} %refs_8_.1) | copy-start | bytes 7684

commit v2 on v1

v2 whole, which is shorter than its diff:
```python
import jax
import jax.numpy as jnp
from jax import lax
from jax.experimental import pallas as pl
from jax.experimental.pallas import tpu as pltpu
from jax.sharding import PartitionSpec as P

NSUB = 3
OFFSETS = ((-1, -1), (-1, 0), (-1, 1), (0, -1), (0, 1), (1, -1), (1, 0), (1, 1))
ORDER = (3, 4, 1, 6, 0, 2, 5, 7)
GROUPS = ((0, 2), (2, 8))
SEND_ORDER = (0, 2, 5, 7, 1, 6, 3, 4)
step_scale = 0.5
MESH = pl.DeviceIdType.MESH
F32 = jnp.float32


def round_up(n, m):
    return (n + m - 1) // m * m


LANES = 128


def tiles_of(ref, width):
    return [ref[:, k * LANES : (k + 1) * LANES] for k in range(width // LANES)]


def spread(index, own, padded):
    return jnp.where(index >= own, index + (padded - own), index)


def kernel(
    n_lat, n_lon, nlev, cells, edges, halo,
    p_in, v_in, ec, ce, sc, se, inv_dual, weight, sound, coupling,
    p_out, v_out,
    pf, vf, p_send, v_send, p_halo, v_halo,
    t_inv, t_low, t_up, work, grad, div,
    p_ss, p_rs, v_ss, v_rs,
):
    a, b = lax.axis_index("lat"), lax.axis_index("lon")
    ecols = vf.shape[1]
    below, above = a > 0, a < n_lat - 1

    def if_there(p, fn):
        if p == 0:
            fn()
        else:
            pl.when(below if p < 0 else above)(fn)

    def target(offset):
        return (a + offset[0], lax.rem(b + offset[1] + n_lon, n_lon))

    p_halo[...] = jnp.zeros_like(p_halo)
    v_halo[...] = jnp.zeros_like(v_halo)

    barrier = pltpu.get_barrier_semaphore()
    for lat_step in (0, -1, 1):
        def greet(lat_step=lat_step):
            for offset in OFFSETS:
                if offset[0] == lat_step:
                    pl.semaphore_signal(
                        barrier, inc=1, device_id=target(offset), device_id_type=MESH
                    )
        if_there(lat_step, greet)

    pf[nlev - nlev % 8 :, :] = jnp.zeros_like(pf[nlev - nlev % 8 :, :])
    pf[0:nlev, :] = p_in[0]
    vf[...] = jnp.zeros_like(vf)
    vf[0:nlev, 0:edges] = v_in[0]
    ccols = pf.shape[1]

    bands = (a + n_lat - 1) // n_lat + (2 * n_lat - 2 - a) // n_lat
    pl.semaphore_wait(barrier, 2 + 3 * bands)

    def copy(member, send, land, ss, rs):
        spot = ORDER.index(7 - member)
        return pltpu.make_async_remote_copy(
            src_ref=send.at[member], dst_ref=land.at[spot],
            send_sem=ss.at[member], recv_sem=rs.at[spot],
            device_id=target(OFFSETS[member]), device_id_type=MESH,
        )

    def launch(tiles, lists, send, land, ss, rs):
        for member in SEND_ORDER:
            send[member] = pick(tiles, range(len(tiles)), lists[0, member : member + 1, :])
            if_there(OFFSETS[member][0], lambda: copy(member, send, land, ss, rs).start())

    def arrive(spot, send, land, ss, rs):
        slot = ORDER[spot]
        if_there(OFFSETS[slot][0], lambda: copy(7 - slot, send, land, ss, rs).wait_recv())

    def retire(send, land, ss, rs):
        for member in range(8):
            if_there(OFFSETS[member][0], lambda: copy(member, send, land, ss, rs).wait_send())

    def add_gradient(tiles, firsts, fresh):
        for k in range(ecols // LANES):
            cols = slice(k * LANES, (k + 1) * LANES)
            taken = [
                pick(tiles, firsts, spread(padded(ec, r, k), cells, ccols)) for r in (0, 1)
            ]
            change = taken[1] - taken[0]
            grad[:, cols] = change if fresh else grad[:, cols] + change

    def add_divergence(tiles, firsts, fresh):
        for k in range(ccols // LANES):
            cols = slice(k * LANES, (k + 1) * LANES)
            total = None if fresh else div[:, cols]
            for j in range(3):
                index = spread(ce[0, j : j + 1, cols], edges, ecols)
                term = pick(tiles, firsts, index) * weight[0, j : j + 1, cols]
                total = term if total is None else total + term
            div[:, cols] = total

    def padded(ref, r, k):
        stop = min(ref.shape[2], (k + 1) * LANES)
        row = ref[0, r : r + 1, k * LANES : stop]
        short = (k + 1) * LANES - stop
        return jnp.pad(row, ((0, 0), (0, short))) if short else row

    def pick(tiles, firsts, index):
        shape = tiles[0].shape
        lane = jnp.broadcast_to(index & (LANES - 1), shape)
        tile = jnp.broadcast_to(index >> 7, shape)
        out = jnp.zeros(shape, F32)
        for values, first in zip(tiles, firsts):
            moved = jnp.take_along_axis(values, lane, axis=1, mode="promise_in_bounds")
            out = jnp.where(tile == first, moved, out)
        return out

    def columns_solved():
        ratio = None
        for level in range(nlev):
            here = coupling[0, level : level + 1, :]
            if level == 0:
                divisor = 1.0 + here
            else:
                lower = coupling[0, level - 1 : level, :]
                divisor = 1.0 + lower + here + lower * ratio
            inverse = 1.0 / divisor
            ratio = -here * inverse
            t_inv[level : level + 1, :] = inverse
            t_up[level : level + 1, :] = ratio
            if level > 0:
                t_low[level : level + 1, :] = lower * inverse

    for substep in range(NSUB):
        own = tiles_of(pf, ccols)
        launch(own, sc, p_send, p_halo, p_ss, p_rs)
        if substep == 0:
            columns_solved()
        add_gradient(own, range(len(own)), True)
        for lo, hi in GROUPS:
            for spot in range(lo, hi):
                arrive(spot, p_send, p_halo, p_ss, p_rs)
            add_gradient(
                [p_halo[spot] for spot in range(lo, hi)],
                [ccols // LANES + ORDER[spot] for spot in range(lo, hi)], False,
            )
        retire(p_send, p_halo, p_ss, p_rs)
        vf[:, 0:edges] = vf[:, 0:edges] - (step_scale * inv_dual[...]) * grad[:, 0:edges]

        own = tiles_of(vf, ecols)
        launch(own, se, v_send, v_halo, v_ss, v_rs)
        add_divergence(own, range(len(own)), True)
        for lo, hi in GROUPS:
            for spot in range(lo, hi):
                arrive(spot, v_send, v_halo, v_ss, v_rs)
            add_divergence(
                [v_halo[spot] for spot in range(lo, hi)],
                [ecols // LANES + ORDER[spot] for spot in range(lo, hi)], False,
            )
        retire(v_send, v_halo, v_ss, v_rs)
        right = pf[...] - sound[...] * div[...]
        work[0:nlev, :] = right[0:nlev] * t_inv[...]

        current = work[0:1, :]
        for level in range(1, nlev):
            current = work[level : level + 1, :] + t_low[level : level + 1, :] * current
            work[level : level + 1, :] = current
        pf[nlev - 1 : nlev, :] = current
        for level in range(nlev - 2, -1, -1):
            current = work[level : level + 1, :] - t_up[level : level + 1, :] * current
            pf[level : level + 1, :] = current

    p_out[0] = pf[0:nlev, :]
    v_out[0] = vf[0:nlev, 0:edges]


def on_device(*args):
    pressure, velocity, send_cells = args[0], args[1], args[4]
    n_lat, n_lon = lax.axis_size("lat"), lax.axis_size("lon")
    nlev, cells, edges = pressure.shape[1], pressure.shape[2], velocity.shape[2]
    halo = send_cells.shape[2]
    rows, ecols = round_up(nlev, 32), round_up(edges, 128)
    vmem = pl.BlockSpec(memory_space=pltpu.VMEM)
    dma8 = pltpu.SemaphoreType.DMA((8,))

    def body(*refs):
        kernel(n_lat, n_lon, nlev, cells, edges, halo, *refs)

    return tuple(pl.pallas_call(
        body,
        name="substeps",
        out_shape=(
            jax.ShapeDtypeStruct(pressure.shape, F32),
            jax.ShapeDtypeStruct(velocity.shape, F32),
        ),
        in_specs=[vmem] * len(args),
        out_specs=(vmem, vmem),
        scratch_shapes=[
            pltpu.VMEM((rows, cells), F32),
            pltpu.VMEM((rows, ecols), F32),
            pltpu.VMEM((8, rows, halo), F32),
            pltpu.VMEM((8, rows, halo), F32),
            pltpu.VMEM((8, rows, halo), F32),
            pltpu.VMEM((8, rows, halo), F32),
            pltpu.VMEM((nlev, cells), F32),
            pltpu.VMEM((nlev, cells), F32),
            pltpu.VMEM((nlev, cells), F32),
            pltpu.VMEM((rows, cells), F32),
            pltpu.VMEM((rows, ecols), F32),
            pltpu.VMEM((rows, cells), F32),
            dma8, dma8, dma8, dma8,
        ],
        compiler_params=pltpu.CompilerParams(collective_id=0, has_side_effects=True, vmem_limit_bytes=40 * 1024 * 1024),
    )(*args))


def solution(mesh):
    band = P("lat", None, "lon")
    flat = P("lat", "lon")
    return jax.shard_map(
        on_device,
        mesh=mesh,
        in_specs=(band, band, band, band, band, band, flat, band, flat, band),
        out_specs=(band, band),
        check_vma=False,
    )
```

time: 43.7 us -> 40.7 us (0.931)
  Pallas kernels: 38.8 us -> 35.8 us
    pallas_call x1, Pallas kernels: 38.8 us -> 35.8 us  [on_device(): pl.pallas_call(body, name='substeps', out_shape=(jax.ShapeDtypeStruct(pre...]
where the time goes in v2:
time: 40.7 us; the launch traced here: 40.4 us
  Pallas kernels  35.8 us (88%)
  local copies, waits for them, and re-layouts  3.85 us (9%)
  between operations  0.73 us (2%)
    pallas_call x1, Pallas kernels, on_device(): pl.pallas_call(body, name='substeps', out_shape=(jax.ShapeDtypeStruct(pre...  35.8 us
    unnamed x21, local copies, waits for them, and re-layouts  2.36 us
    pallas_call x2, local copies, waits for them, and re-layouts, on_device(): pl.pallas_call(body, name='substeps', out_shape=(jax.ShapeDtypeStruct(pre...  1.49 us

profile of v2, /device:TPU:0, one launch (start us, length us, event | category | flops | bytes accessed | tf_op | source)
XLA Modules:
  0.0 40.4 jit_solution(2252806777834646652)
XLA Ops:
  0.6 0.0 copy-start.7
  0.6 0.7 %copy.14.refs_3_ = s32[1,3,640]{2,1,0:T(4,128)S(1)} copy(s32[1,3,640]{2,0,1:T(1,128)} %param.13) | data formatting | bytes 15360 | tf_op args[3]
  1.3 0.0 copy-done.7
  1.3 0.0 copy-start.6
  1.4 0.0 copy-start.5
  1.4 0.9 %copy.12.refs_0_ = f32[1,30,640]{2,1,0:T(8,128)S(1)} copy(f32[1,30,640]{2,0,1:T(1,128)} %param.10) | data formatting | bytes 153600 | tf_op args[0]
  2.3 0.0 copy-done.6
  2.3 0.0 copy-done.5
  2.3 0.0 copy-start
  2.3 0.0 copy-start.1
  2.4 0.0 copy-start.2
  2.4 0.0 copy-start.3
  2.4 0.0 copy-start.4
  2.4 0.6 %copy-done = s32[1,2,960]{2,1,0:T(2,128)S(1)} copy-done((s32[1,2,960]{2,1,0:T(2,128)S(1)}, s32[1,2,960]{2,1,0:T(2,128)}, u32[]{:S(2)}) %copy-start) | copy-done | bytes 7704
  3.0 0.0 copy-done.1
  3.0 0.0 copy-done.2
  3.1 0.0 copy-done.3
  3.1 0.0 copy-done.4
  3.1 35.8 %substeps.1 = (f32[1,30,640]{2,1,0:T(8,128)S(1)}, f32[1,30,960]{2,1,0:T(8,128)S(1)}) custom-call(f32[1,30,640]{2,1,0:T(8,128)S(1)} %copy.12.refs_0_, f32[1,30,960]{2,1,0:T(8,128)S(1)} %copy.13.refs_1_, s32[1,2,960]{2,1,0:T(2,128)S(1)} %copy-done, s32[1,3,640]{2,1,0:T(4,128)S(1)} %copy.14.refs_3_, s32[1,8,128]{2,1,0:T(8,128)S(1)} %copy-done.1, ...), custom_call_target="tpu_custom_call" | custom-call | tf_op jit(solution)/shard_map/substeps/pallas_call | solution.py:203
  38.9 0.7 %copy.17 = f32[1,30,640]{2,0,1:T(1,128)} copy(f32[1,30,640]{2,1,0:T(8,128)S(1)} %get-tuple-element.2) | data formatting | bytes 153600 | tf_op jit(solution)/shard_map/substeps/pallas_call | solution.py:203
  39.6 0.8 %copy.18 = f32[1,30,960]{2,0,1:T(1,128)} copy(f32[1,30,960]{2,1,0:T(8,128)S(1)} %get-tuple-element.3) | data formatting | bytes 230400 | tf_op jit(solution)/shard_map/substeps/pallas_call | solution.py:203
  (3 shorter events, 0.0 us)
Async XLA Ops:
  0.6 0.7 %copy-start.7 = (f32[1,3,640]{2,0,1:T(1,128)S(1)}, f32[1,3,640]{2,0,1:T(1,128)}, u32[]{:S(2)}) copy-start(f32[1,3,640]{2,0,1:T(1,128)} %param.17) | copy-start | bytes 23044
  1.3 1.0 %copy-start.6 = (f32[1,30,640]{2,0,1:T(1,128)S(1)}, f32[1,30,640]{2,0,1:T(1,128)}, u32[]{:S(2)}) copy-start(f32[1,30,640]{2,0,1:T(1,128)} %param.19) | copy-start | bytes 230404
  1.4 1.0 %copy-start.5 = (f32[1,30,960]{2,0,1:T(1,128)S(1)}, f32[1,30,960]{2,0,1:T(1,128)}, u32[]{:S(2)}) copy-start(f32[1,30,960]{2,0,1:T(1,128)} %param.11) | copy-start | bytes 345604
  2.3 0.7 %copy-start = (s32[1,2,960]{2,1,0:T(2,128)S(1)}, s32[1,2,960]{2,1,0:T(2,128)}, u32[]{:S(2)}) copy-start(s32[1,2,960]{2,1,0:T(2,128)} %refs_2_.1) | copy-start | bytes 23044
  2.3 0.7 %copy-start.1 = (s32[1,8,128]{2,1,0:T(8,128)S(1)}, s32[1,8,128]{2,1,0:T(8,128)}, u32[]{:S(2)}) copy-start(s32[1,8,128]{2,1,0:T(8,128)} %refs_4_.1) | copy-start | bytes 12292
  2.4 0.7 %copy-start.2 = (s32[1,8,128]{2,1,0:T(8,128)S(1)}, s32[1,8,128]{2,1,0:T(8,128)}, u32[]{:S(2)}) copy-start(s32[1,8,128]{2,1,0:T(8,128)} %refs_5_.1) | copy-start | bytes 12292
  2.4 0.7 %copy-start.3 = (f32[1,960]{1,0:T(1,128)S(1)}, f32[1,960]{1,0:T(1,128)}, u32[]{:S(2)}) copy-start(f32[1,960]{1,0:T(1,128)} %refs_6_.1) | copy-start | bytes 11524
  2.4 0.7 %copy-start.4 = (f32[1,640]{1,0:T(1,128)S(1)}, f32[1,640]{1,0:T(1,128)}, u32[]{:S(2)}) copy-start(f32[1,640]{1,0:T(1,128)} %refs_8_.1) | copy-start | bytes 7684

commit v3 on v2

v3 whole, which is shorter than its diff:
```python
import jax
import jax.numpy as jnp
from jax import lax
from jax.experimental import pallas as pl
from jax.experimental.pallas import tpu as pltpu
from jax.sharding import PartitionSpec as P

NSUB = 3
OFFSETS = ((-1, -1), (-1, 0), (-1, 1), (0, -1), (0, 1), (1, -1), (1, 0), (1, 1))
LANES = 128
step_scale = 0.5
MESH = pl.DeviceIdType.MESH
F32 = jnp.float32


def round_up(n, m):
    return (n + m - 1) // m * m


def tiles_of(ref, width):
    return [ref[:, k * LANES : (k + 1) * LANES] for k in range(width // LANES)]


def spread(index, own, padded):
    return jnp.where(index >= own, index + (padded - own), index)


def member_of(p, q):
    return (1 + q, 3 + (q + 1) // 2, 6 + q)[p + 1]


def kernel(
    n_lat, n_lon, nlev, cells, edges, halo,
    p_hbm, v_hbm, ec_hbm, ce_hbm, sc_hbm, se_hbm, inv_hbm, weight_hbm, sound_hbm, coupling_hbm,
    p_out, v_out,
    p_row, v_row, ec, ce, sc, se, inv_dual, weight, sound, coupling,
    pf, vf, p_send, v_send, p_halo, v_halo,
    t_inv, t_low, t_up, work, grad, div,
    p_ss, p_rs, v_ss, v_rs, in_sem, out_sem,
):
    a, b = lax.axis_index("lat"), lax.axis_index("lon")
    ccols, ecols = pf.shape[1], vf.shape[1]
    below, above = a > 0, a < n_lat - 1
    far = 2 * ((2 * b) // n_lon) - 1
    near = -far
    sends = [(-1, far), (1, far), (0, far), (-1, 0), (1, 0), (-1, near), (1, near), (0, near)]
    arrivals = [[(0, near), (-1, 0), (1, 0)], [(-1, near), (1, near), (0, far)], [(-1, far), (1, far)]]

    def if_there(p, fn):
        if p == 0:
            fn()
        else:
            pl.when(below if p < 0 else above)(fn)

    def target(p, q):
        return (a + p, lax.rem(b + q + n_lon, n_lon))

    barrier = pltpu.get_barrier_semaphore()
    for lat_step in (-1, 1, 0):
        def greet(lat_step=lat_step):
            for offset in OFFSETS:
                if offset[0] == lat_step:
                    pl.semaphore_signal(
                        barrier, inc=1, device_id=target(*offset), device_id_type=MESH
                    )
        if_there(lat_step, greet)

    pairs = [
        (coupling_hbm, coupling), (p_hbm, p_row), (sc_hbm, sc), (ec_hbm, ec), (v_hbm, v_row),
        (inv_hbm, inv_dual), (se_hbm, se), (ce_hbm, ce), (weight_hbm, weight), (sound_hbm, sound),
    ]
    loads = [pltpu.make_async_copy(x, y, in_sem.at[k]) for k, (x, y) in enumerate(pairs)]
    for load in loads:
        load.start()

    def clear(p):
        def fill():
            for slot, offset in enumerate(OFFSETS):
                if offset[0] == p:
                    p_halo[slot] = jnp.zeros(p_halo.shape[1:], F32)
                    v_halo[slot] = jnp.zeros(v_halo.shape[1:], F32)
        return fill

    pl.when(a == 0)(clear(-1))
    pl.when(a == n_lat - 1)(clear(1))
    pf[nlev - nlev % 8 :, :] = jnp.zeros_like(pf[nlev - nlev % 8 :, :])
    vf[...] = jnp.zeros_like(vf)

    def copy(p, q, send, land, ss, rs):
        member = member_of(p, q)
        return pltpu.make_async_remote_copy(
            src_ref=send.at[member], dst_ref=land.at[7 - member],
            send_sem=ss.at[member], recv_sem=rs.at[7 - member],
            device_id=target(p, q), device_id_type=MESH,
        )

    def collect(tiles, lists, send, offsets):
        for p, q in offsets:
            index = lists[0, pl.ds(member_of(p, q), 1), :]
            send[member_of(p, q)] = pick(tiles, range(len(tiles)), index)

    def launch(offsets, *refs):
        for p, q in offsets:
            if_there(p, lambda: copy(p, q, *refs).start())

    def arrive(group, *refs):
        for p, q in group:
            if_there(p, lambda: copy(-p, -q, *refs).wait_recv())

    def retire(*refs):
        for p, q in sends:
            if_there(p, lambda: copy(p, q, *refs).wait_send())

    def pick(tiles, firsts, index):
        shape = tiles[0].shape
        lane = jnp.broadcast_to(index & (LANES - 1), shape)
        tile = jnp.broadcast_to(index >> 7, shape)
        out = jnp.zeros(shape, F32)
        for values, first in zip(tiles, firsts):
            moved = jnp.take_along_axis(values, lane, axis=1, mode="promise_in_bounds")
            out = jnp.where(tile == first, moved, out)
        return out

    def halo_tiles(land, group, own):
        slots = [member_of(p, q) for p, q in group]
        return [land[slot] for slot in slots], [own + slot for slot in slots]

    def edge_columns(ref, row, k):
        stop = min(edges, (k + 1) * LANES)
        part = row(ref)[:, k * LANES : stop]
        short = (k + 1) * LANES - stop
        return jnp.pad(part, ((0, 0), (0, short))) if short else part

    def add_gradient(tiles, firsts, fresh, last):
        for k in range(ecols // LANES):
            cols = slice(k * LANES, (k + 1) * LANES)
            taken = [
                pick(tiles, firsts, spread(edge_columns(ec, lambda ref: ref[0, r : r + 1, :], k), cells, ccols))
                for r in (0, 1)
            ]
            change = taken[1] - taken[0]
            total = change if fresh else grad[:, cols] + change
            if last:
                scale = step_scale * edge_columns(inv_dual, lambda ref: ref[...], k)
                vf[:, cols] = vf[:, cols] - scale * total
            else:
                grad[:, cols] = total

    def add_divergence(tiles, firsts, fresh, last):
        for k in range(ccols // LANES):
            cols = slice(k * LANES, (k + 1) * LANES)
            total = None if fresh else div[:, cols]
            for j in range(3):
                term = pick(tiles, firsts, spread(ce[j, :, cols], edges, ecols)) * weight[j, :, cols]
                total = term if total is None else total + term
            if last:
                right = pf[:, cols] - sound[:, cols] * total
                work[0:nlev, cols] = right[0:nlev] * t_inv[:, cols]
            else:
                div[:, cols] = total

    def columns_solved():
        ratio = None
        for level in range(nlev):
            here = coupling[level]
            if level == 0:
                divisor = 1.0 + here
            else:
                lower = coupling[level - 1]
                divisor = 1.0 + lower + here + lower * ratio
            inverse = 1.0 / divisor
            ratio = -here * inverse
            t_inv[level : level + 1, :] = inverse
            t_up[level : level + 1, :] = ratio
            if level > 0:
                t_low[level : level + 1, :] = lower * inverse

    p_refs = (p_send, p_halo, p_ss, p_rs)
    v_refs = (v_send, v_halo, v_ss, v_rs)
    for load in loads[:3]:
        load.wait()
    for level in range(nlev):
        pf[level : level + 1, :] = p_row[level]
    own = tiles_of(pf, ccols)
    collect(own, sc, p_send, sends)
    columns_solved()
    bands = (a + n_lat - 1) // n_lat + (2 * n_lat - 2 - a) // n_lat
    pl.semaphore_wait(barrier, 2 + 3 * bands)

    for substep in range(NSUB):
        final = substep == NSUB - 1
        if substep == 0:
            launch(sends, *p_refs)
            for load in loads[3:]:
                load.wait()
            for level in range(nlev):
                vf[level : level + 1, 0:edges] = v_row[level]
        else:
            own = tiles_of(pf, ccols)
            for part in (sends[:3], sends[3:]):
                collect(own, sc, p_send, part)
                launch(part, *p_refs)
        add_gradient(own, range(len(own)), True, False)
        for k, group in enumerate(arrivals):
            arrive(group, *p_refs)
            add_gradient(*halo_tiles(p_halo, group, ccols // LANES), False, k == 2)
        retire(*p_refs)

        own = tiles_of(vf, ecols)
        for part in (sends[:3], sends[3:]):
            collect(own, se, v_send, part)
            launch(part, *v_refs)
        if final:
            for level in range(nlev):
                v_row[level] = vf[level : level + 1, 0:edges]
            v_store = pltpu.make_async_copy(v_row, v_out, out_sem.at[0])
            v_store.start()
        add_divergence(own, range(len(own)), True, False)
        for k, group in enumerate(arrivals):
            arrive(group, *v_refs)
            add_divergence(*halo_tiles(v_halo, group, ecols // LANES), False, k == 2)
        retire(*v_refs)

        current = work[0:1, :]
        for level in range(1, nlev):
            current = work[level : level + 1, :] + t_low[level : level + 1, :] * current
            work[level : level + 1, :] = current
        for level in range(nlev - 1, -1, -1):
            if level < nlev - 1:
                current = work[level : level + 1, :] - t_up[level : level + 1, :] * current
            if final:
                p_row[level] = current
            else:
                pf[level : level + 1, :] = current

    p_store = pltpu.make_async_copy(p_row, p_out, out_sem.at[1])
    p_store.start()
    p_store.wait()
    v_store.wait()


def level_major(x):
    return jnp.transpose(x, (1, 0, 2))


def on_device(*args):
    pressure, velocity, send_cells = args[0], args[1], args[4]
    n_lat, n_lon = lax.axis_size("lat"), lax.axis_size("lon")
    nlev, cells, edges = pressure.shape[1], pressure.shape[2], velocity.shape[2]
    halo = send_cells.shape[2]
    rows, ecols = round_up(nlev, 32), round_up(edges, 128)
    hbm = pl.BlockSpec(memory_space=pltpu.HBM)
    dma8 = pltpu.SemaphoreType.DMA((8,))
    args = [level_major(x) if k in (0, 1, 3, 7, 9) else x for k, x in enumerate(args)]

    def body(*refs):
        kernel(n_lat, n_lon, nlev, cells, edges, halo, *refs)

    halo_shape = pltpu.VMEM((8, rows, halo), F32)
    cell_shape = pltpu.VMEM((rows, cells), F32)
    edge_shape = pltpu.VMEM((rows, ecols), F32)
    level_shape = pltpu.VMEM((nlev, cells), F32)
    outs = pl.pallas_call(
        body,
        name="substeps",
        out_shape=(
            jax.ShapeDtypeStruct(args[0].shape, F32),
            jax.ShapeDtypeStruct(args[1].shape, F32),
        ),
        in_specs=[hbm] * len(args),
        out_specs=(hbm, hbm),
        scratch_shapes=[pltpu.VMEM(x.shape, x.dtype) for x in args] + [
            cell_shape, edge_shape, halo_shape, halo_shape, halo_shape, halo_shape,
            level_shape, level_shape, level_shape, cell_shape, edge_shape, cell_shape,
            dma8, dma8, dma8, dma8,
            pltpu.SemaphoreType.DMA((len(args),)), pltpu.SemaphoreType.DMA((2,)),
        ],
        compiler_params=pltpu.CompilerParams(
            collective_id=0, has_side_effects=True, vmem_limit_bytes=67_000_000
        ),
    )(*args)
    return tuple(level_major(x) for x in outs)


def solution(mesh):
    band = P("lat", None, "lon")
    flat = P("lat", "lon")
    return jax.shard_map(
        on_device,
        mesh=mesh,
        in_specs=(band, band, band, band, band, band, flat, band, flat, band),
        out_specs=(band, band),
        check_vma=False,
    )
```

time: 40.7 us -> 38.6 us (0.948)
  local copies, waits for them, and re-layouts: 3.85 us -> 2.23 us
    pallas_call x2 -> x0, local copies, waits for them, and re-layouts: 1.49 us -> none  [on_device(): pl.pallas_call(body, name='substeps', out_shape=(jax.ShapeDtypeStruct(pre...]
    unnamed x21 -> x4, local copies, waits for them, and re-layouts: 2.36 us -> 2.23 us
where the time goes in v3:
time: 38.6 us; the launch traced here: 38.4 us
  Pallas kernels  35.6 us (92%)
  local copies, waits for them, and re-layouts  2.23 us (6%)
  between operations  0.65 us (2%)
    pallas_call x1, Pallas kernels, on_device(): pl.pallas_call(body, name='substeps', out_shape=(jax.ShapeDtypeStruct(arg...  35.6 us
    unnamed x4, local copies, waits for them, and re-layouts  2.23 us

profile of v3, /device:TPU:0, one launch (start us, length us, event | category | flops | bytes accessed | tf_op | source)
XLA Modules:
  0.0 38.4 jit_solution(1372442020375064)
XLA Ops:
  0.6 35.6 %substeps.1 = (f32[30,1,640]{2,1,0:T(1,128)}, f32[30,1,960]{2,1,0:T(1,128)}) custom-call(f32[30,1,640]{2,1,0:T(1,128)} %bitcast.9, f32[30,1,960]{2,1,0:T(1,128)} %bitcast.7, s32[1,2,960]{2,1,0:T(2,128)} %refs_2_.1, s32[3,1,640]{2,1,0:T(1,128)} %bitcast.12, s32[1,8,128]{2,1,0:T(8,128)} %refs_4_.1, s32[1,8,128]{2,1,0:T(8,128)} %refs_5_.1, f32[1,960]{1,0:T(1,128)} %refs_6_.1, ...), custom_call_target="tpu_custom_call" | custom-call | tf_op jit(solution)/shard_map/substeps/pallas_call | solution.py:263
  36.2 0.0 copy-start
  36.2 1.6 %copy.14 = f32[1,30,640]{2,0,1:T(1,128)} copy(f32[1,30,640]{2,0,1:T(1,128)} %bitcast.11) | data formatting | bytes 153600
  37.8 0.0 copy-done
  37.8 0.6 %copy.15 = f32[1,30,960]{2,0,1:T(1,128)} copy(f32[1,30,960]{2,0,1:T(1,128)S(1)} %bitcast.8) | data formatting | bytes 230400
Async XLA Ops:
  36.2 1.6 %copy-start = (f32[30,1,960]{2,1,0:T(1,128)S(1)}, f32[30,1,960]{2,1,0:T(1,128)}, u32[]{:S(2)}) copy-start(f32[30,1,960]{2,1,0:T(1,128)} %get-tuple-element.5) | copy-start | bytes 345604

commit v4 on v3

--- a/solution.py
+++ b/solution.py
@@ -36,7 +36,7 @@
     p_row, v_row, ec, ce, sc, se, inv_dual, weight, sound, coupling,
     pf, vf, p_send, v_send, p_halo, v_halo,
     t_inv, t_low, t_up, work, grad, div,
-    p_ss, p_rs, v_ss, v_rs, in_sem, out_sem,
+    p_ss, p_rs, v_ss, v_rs, in_sem,
 ):
     a, b = lax.axis_index("lat"), lax.axis_index("lon")
     ccols, ecols = pf.shape[1], vf.shape[1]
@@ -44,7 +44,7 @@
     far = 2 * ((2 * b) // n_lon) - 1
     near = -far
     sends = [(-1, far), (1, far), (0, far), (-1, 0), (1, 0), (-1, near), (1, near), (0, near)]
-    arrivals = [[(0, near), (-1, 0), (1, 0)], [(-1, near), (1, near), (0, far)], [(-1, far), (1, far)]]
+    arrivals = [[(0, near), (-1, 0), (1, 0), (-1, near), (1, near), (0, far)], [(-1, far), (1, far)]]
 
     def if_there(p, fn):
         if p == 0:
@@ -203,7 +203,7 @@
         add_gradient(own, range(len(own)), True, False)
         for k, group in enumerate(arrivals):
             arrive(group, *p_refs)
-            add_gradient(*halo_tiles(p_halo, group, ccols // LANES), False, k == 2)
+            add_gradient(*halo_tiles(p_halo, group, ccols // LANES), False, k == 1)
         retire(*p_refs)
 
         own = tiles_of(vf, ecols)
@@ -212,13 +212,11 @@
             launch(part, *v_refs)
         if final:
             for level in range(nlev):
-                v_row[level] = vf[level : level + 1, 0:edges]
-            v_store = pltpu.make_async_copy(v_row, v_out, out_sem.at[0])
-            v_store.start()
+                v_out[level] = vf[level : level + 1, 0:edges]
         add_divergence(own, range(len(own)), True, False)
         for k, group in enumerate(arrivals):
             arrive(group, *v_refs)
-            add_divergence(*halo_tiles(v_halo, group, ecols // LANES), False, k == 2)
+            add_divergence(*halo_tiles(v_halo, group, ecols // LANES), False, k == 1)
         retire(*v_refs)
 
         current = work[0:1, :]
@@ -229,14 +227,20 @@
             if level < nlev - 1:
                 current = work[level : level + 1, :] - t_up[level : level + 1, :] * current
             if final:
-                p_row[level] = current
+                p_out[level] = current
             else:
                 pf[level : level + 1, :] = current
 
-    p_store = pltpu.make_async_copy(p_row, p_out, out_sem.at[1])
-    p_store.start()
-    p_store.wait()
-    v_store.wait()
+
+def write_out(p_ref, v_ref, p_out, v_out, sem):
+    stores = [
+        pltpu.make_async_copy(x, y, sem.at[k])
+        for k, (x, y) in enumerate(((v_ref, v_out), (p_ref, p_out)))
+    ]
+    for store in stores:
+        store.start()
+    for store in stores:
+        store.wait()
 
 
 def level_major(x):
@@ -250,6 +254,7 @@
     halo = send_cells.shape[2]
     rows, ecols = round_up(nlev, 32), round_up(edges, 128)
     hbm = pl.BlockSpec(memory_space=pltpu.HBM)
+    vmem = pl.BlockSpec(memory_space=pltpu.VMEM)
     dma8 = pltpu.SemaphoreType.DMA((8,))
     args = [level_major(x) if k in (0, 1, 3, 7, 9) else x for k, x in enumerate(args)]
 
@@ -264,21 +269,30 @@
         body,
         name="substeps",
         out_shape=(
-            jax.ShapeDtypeStruct(args[0].shape, F32),
-            jax.ShapeDtypeStruct(args[1].shape, F32),
+            pltpu.VMEM(args[0].shape, F32),
+            pltpu.VMEM(args[1].shape, F32),
         ),
         in_specs=[hbm] * len(args),
-        out_specs=(hbm, hbm),
+        out_specs=(vmem, vmem),
         scratch_shapes=[pltpu.VMEM(x.shape, x.dtype) for x in args] + [
             cell_shape, edge_shape, halo_shape, halo_shape, halo_shape, halo_shape,
             level_shape, level_shape, level_shape, cell_shape, edge_shape, cell_shape,
             dma8, dma8, dma8, dma8,
-            pltpu.SemaphoreType.DMA((len(args),)), pltpu.SemaphoreType.DMA((2,)),
+            pltpu.SemaphoreType.DMA((len(args),)),
         ],
         compiler_params=pltpu.CompilerParams(
-            collective_id=0, has_side_effects=True, vmem_limit_bytes=67_000_000
+            collective_id=0, has_side_effects=True, vmem_limit_bytes=66_000_000
         ),
     )(*args)
+    outs = pl.pallas_call(
+        write_out,
+        name="write_out",
+        out_shape=tuple(jax.ShapeDtypeStruct(x.shape, F32) for x in outs),
+        in_specs=[vmem] * 2,
+        out_specs=(hbm, hbm),
+        scratch_shapes=[pltpu.SemaphoreType.DMA((2,))],
+        compiler_params=pltpu.CompilerParams(vmem_limit_bytes=1024 * 1024),
+    )(*outs)
     return tuple(level_major(x) for x in outs)
 
 

time: 38.6 us -> 35.6 us (0.922)
  local copies, waits for them, and re-layouts: 2.23 us -> 0 us
  Pallas kernels: 35.6 us -> 34.8 us
    unnamed x4 -> x0, local copies, waits for them, and re-layouts: 2.23 us -> none
    pallas_call x1 -> x2, Pallas kernels: 35.6 us -> 34.8 us  [the longest x1 34.1 us: on_device(): pl.pallas_call(body, name='substeps', out_shape=(pltpu.VMEM(args[0].shape...]
where the time goes in v4:
time: 35.6 us; the launch traced here: 35.4 us
  Pallas kernels  34.8 us (98%)
  between operations  0.64 us (2%)
    pallas_call x1, Pallas kernels, on_device(): pl.pallas_call(body, name='substeps', out_shape=(pltpu.VMEM(args[0].shape...  34.1 us

profile of v4, /device:TPU:0, one launch (start us, length us, event | category | flops | bytes accessed | tf_op | source)
XLA Modules:
  0.0 35.4 jit_solution(16438888757806264797)
XLA Ops:
  0.6 34.1 %substeps.1 = (f32[30,1,640]{2,1,0:T(1,128)S(1)}, f32[30,1,960]{2,1,0:T(1,128)S(1)}) custom-call(f32[30,1,640]{2,1,0:T(1,128)} %bitcast.8, f32[30,1,960]{2,1,0:T(1,128)} %bitcast.7, s32[1,2,960]{2,1,0:T(2,128)} %refs_2_.1, s32[3,1,640]{2,1,0:T(1,128)} %bitcast.10, s32[1,8,128]{2,1,0:T(8,128)} %refs_4_.1, s32[1,8,128]{2,1,0:T(8,128)} %refs_5_.1, ...), custom_call_target="tpu_custom_call" | custom-call | tf_op jit(solution)/shard_map/substeps/pallas_call | solution.py:268
  34.7 0.7 %write_out.1 = (f32[30,1,640]{2,1,0:T(1,128)}, f32[30,1,960]{2,1,0:T(1,128)}) custom-call(f32[30,1,640]{2,1,0:T(1,128)S(1)} %get-tuple-element.6.p_ref, f32[30,1,960]{2,1,0:T(1,128)S(1)} %get-tuple-element.7.v_ref), custom_call_target="tpu_custom_call" | custom-call | tf_op jit(solution)/shard_map/write_out/pallas_call | solution.py:287

commit v5 on v4

--- a/solution.py
+++ b/solution.py
@@ -201,10 +201,11 @@
                 collect(own, sc, p_send, part)
                 launch(part, *p_refs)
         add_gradient(own, range(len(own)), True, False)
+        if substep > 0:
+            retire(*v_refs)
         for k, group in enumerate(arrivals):
             arrive(group, *p_refs)
             add_gradient(*halo_tiles(p_halo, group, ccols // LANES), False, k == 1)
-        retire(*p_refs)
 
         own = tiles_of(vf, ecols)
         for part in (sends[:3], sends[3:]):
@@ -214,10 +215,10 @@
             for level in range(nlev):
                 v_out[level] = vf[level : level + 1, 0:edges]
         add_divergence(own, range(len(own)), True, False)
+        retire(*p_refs)
         for k, group in enumerate(arrivals):
             arrive(group, *v_refs)
             add_divergence(*halo_tiles(v_halo, group, ecols // LANES), False, k == 1)
-        retire(*v_refs)
 
         current = work[0:1, :]
         for level in range(1, nlev):
@@ -230,6 +231,8 @@
                 p_out[level] = current
             else:
                 pf[level : level + 1, :] = current
+
+    retire(*v_refs)
 
 
 def write_out(p_ref, v_ref, p_out, v_out, sem):

time: 35.6 us -> 35.4 us (level)
  no operation moved by 1% of the time
where the time goes in v5:
time: 35.4 us; the launch traced here: 35.3 us
  Pallas kernels  34.6 us (98%)
  between operations  0.64 us (2%)
    pallas_call x1, Pallas kernels, on_device(): pl.pallas_call(body, name='substeps', out_shape=(pltpu.VMEM(args[0].shape...  33.9 us

profile of v5, /device:TPU:0, one launch (start us, length us, event | category | flops | bytes accessed | tf_op | source)
XLA Modules:
  0.0 35.3 jit_solution(40665829855898827)
XLA Ops:
  0.6 33.9 %substeps.1 = (f32[30,1,640]{2,1,0:T(1,128)S(1)}, f32[30,1,960]{2,1,0:T(1,128)S(1)}) custom-call(f32[30,1,640]{2,1,0:T(1,128)} %bitcast.8, f32[30,1,960]{2,1,0:T(1,128)} %bitcast.7, s32[1,2,960]{2,1,0:T(2,128)} %refs_2_.1, s32[3,1,640]{2,1,0:T(1,128)} %bitcast.10, s32[1,8,128]{2,1,0:T(8,128)} %refs_4_.1, s32[1,8,128]{2,1,0:T(8,128)} %refs_5_.1, ...), custom_call_target="tpu_custom_call" | custom-call | tf_op jit(solution)/shard_map/substeps/pallas_call | solution.py:271
  34.6 0.7 %write_out.1 = (f32[30,1,640]{2,1,0:T(1,128)}, f32[30,1,960]{2,1,0:T(1,128)}) custom-call(f32[30,1,640]{2,1,0:T(1,128)S(1)} %get-tuple-element.6.p_ref, f32[30,1,960]{2,1,0:T(1,128)S(1)} %get-tuple-element.7.v_ref), custom_call_target="tpu_custom_call" | custom-call | tf_op jit(solution)/shard_map/write_out/pallas_call | solution.py:290
